TPU v7x, 32 devices: a whole 2x2x4 slice. The times are simulated.
32 devices in a mesh: case: 2 (over x), model: 4 (over z), ens: 4 (over y, core).
Axes of the slice: x: 2, y: 2, z: 4, core: 2. Of those that a mesh axis runs over, the one named last changes fastest.
Arguments:
- ens_init: float32 [64, 2048, 48], P(('case', 'ens'), None, 'model'), parts along dimension 0
- mix_op: bfloat16 [2048, 2048], replicated
- w_in: bfloat16 [3, 48, 768], P(None, None, 'model')
- w_out: bfloat16 [3, 768, 48], P(None, 'model')
- obs_val: float32 [3, 4096, 12], P(None, ('case', 'ens', 'model')), parts along dimension 1
- obs_prec: float32 [4096, 12], P(('case', 'ens', 'model')), parts along dimension 0
- obs_idx: int32 [12], replicated
- inflation: float32 [1], replicated
Outputs:
- output: float32 [64, 2048, 48], P(('case', 'ens'), None, 'model'), parts along dimension 0
There are 2 independent parts. A program takes and returns all parts, laid end to end along the dimension named above; an argument that names none is the same for every part.
All inputs are finite; a program needn't handle non-finite values.
Results may differ from a plain program's by a relative error of at most 0.0173175.
Values are sent between devices in bfloat16 or wider.
A program may use at most 1 GiB of HBM per device.

v0:
```python
import jax
import jax.numpy as jnp
from jax import lax
from jax.sharding import PartitionSpec as P

NS_STEPS = 12
FULL_PREC = lax.Precision.HIGHEST


def value_a8(ens_state, mix_op, w_in, w_out):
    for layer_idx in range(w_in.shape[0]):
        mix_out = jnp.einsum('ij,jkc->ikc', mix_op, ens_state.astype(jnp.bfloat16), preferred_element_type=jnp.float32).astype(jnp.bfloat16)
        mix_full = lax.all_gather(mix_out, 'model', axis=2, tiled=True)
        hidden = jax.nn.gelu(jnp.einsum('ikv,vf->ikf', mix_full, w_in[layer_idx], preferred_element_type=jnp.float32), approximate=True)
        part_sum = jnp.einsum('ikf,fv->ikv', hidden.astype(jnp.bfloat16), w_out[layer_idx], preferred_element_type=jnp.float32)
        ens_state = ens_state + lax.psum_scatter(part_sum, 'model', scatter_dimension=2, tiled=True)
    return ens_state


def letkf_weights(col_state, obs_now, prec_now, obs_idx, inflation):
    members = col_state.shape[-2]
    ens_mean = jnp.mean(col_state, axis=-2)
    anomaly = col_state - ens_mean[..., None, :]
    obs_anom = jnp.take(anomaly, obs_idx, axis=-1)
    innovation = obs_now - jnp.take(ens_mean, obs_idx, axis=-1)
    weighted = obs_anom * prec_now[..., None, :]
    identity = jnp.eye(members, dtype=jnp.float32)
    a_tilde = ((members - 1) / inflation[0]) * identity + jnp.einsum('...ip,...jp->...ij', weighted, obs_anom, precision=FULL_PREC)
    trace_sum = jnp.trace(a_tilde, axis1=-2, axis2=-1)[..., None, None]
    b_mat = a_tilde / trace_sum
    t_mat = 1.5 * identity - 0.5 * b_mat
    z_mat = t_mat
    for ns_step in range(1, NS_STEPS):
        b_mat = jnp.matmul(b_mat, t_mat, precision=FULL_PREC)
        t_mat = 1.5 * identity - 0.5 * jnp.matmul(z_mat, b_mat, precision=FULL_PREC)
        z_mat = jnp.matmul(t_mat, z_mat, precision=FULL_PREC)
    sqrt_inv = z_mat / jnp.sqrt(trace_sum)
    gain_vec = jnp.einsum('...ip,...p->...i', weighted, innovation, precision=FULL_PREC)
    half_step = jnp.einsum('...ij,...j->...i', sqrt_inv, gain_vec, precision=FULL_PREC)
    w_mean = jnp.einsum('...ij,...j->...i', sqrt_inv, half_step, precision=FULL_PREC)
    w_full = (members - 1) ** 0.5 * sqrt_inv + w_mean[..., None]
    return ens_mean, anomaly, w_full


def solution(mesh):
    def local_step(ens_local, mix_op, w_in, w_out, obs_val, obs_prec, obs_idx, inflation):
        ens_state = jnp.transpose(ens_local, (1, 0, 2))
        for cycle_idx in range(obs_val.shape[0]):
            ens_state = value_a8(ens_state, mix_op, w_in, w_out)
            col_state = lax.all_to_all(ens_state, 'ens', 0, 1, tiled=True)
            col_state = lax.all_to_all(col_state, 'model', 0, 2, tiled=True)
            ens_mean, anomaly, w_full = letkf_weights(col_state, obs_val[cycle_idx], obs_prec, obs_idx, inflation)
            col_state = ens_mean[:, None, :] + jnp.einsum('bik,biv->bkv', w_full, anomaly, precision=FULL_PREC)
            col_state = lax.all_to_all(col_state, 'model', 2, 0, tiled=True)
            ens_state = lax.all_to_all(col_state, 'ens', 1, 0, tiled=True)
        return jnp.transpose(ens_state, (1, 0, 2))

    member_spec = P(('case', 'ens'), None, 'model')
    col_axes = ('case', 'ens', 'model')
    in_specs = (member_spec, P(None, None), P(None, None, 'model'), P(None, 'model', None), P(None, col_axes, None), P(col_axes, None), P(None), P(None))
    return jax.shard_map(local_step, mesh=mesh, in_specs=in_specs, out_specs=member_spec, check_vma=False)
```

profile of v0, /device:TPU:2, one launch (start us, length us, event | category | flops | bytes accessed | tf_op | source)
XLA Modules:
  0.0 1833.3 jit_solution(3714762852090714416)
XLA Ops:
  7.7 6.4 fusion.150
  15.2 38.0 %all-gather.10.cloned.1.call-done = bf16[2048,8,48]{0,1,2:T(8,128)(2,1)} async-done(((bf16[2048,8,12]{0,1,2:T(8,128)(2,1)}), bf16[2048,8,48]{0,1,2:T(8,128)(2,1)}) %all-gather.10.cloned.1.call-update) | async-done | bytes 1572880 | tf_op jit(solution)/shard_map/all_gather | solution.py:13
  53.2 7.2 fusion.106
  64.2 59.5 %reduce-scatter.10.cloned.1.call-done = f32[2048,8,12]{0,1,2:T(8,128)} async-done(((f32[2048,8,48]{0,1,2:T(8,128)}), f32[2048,8,12]{0,1,2:T(8,128)}) %reduce-scatter.10.cloned.1.call-update) | async-done | bytes 786448 | tf_op jit(solution)/shard_map/reduce_scatter | solution.py:16
  124.9 6.4 fusion.174
  132.3 36.5 %all-gather.12.cloned.1.call-done = bf16[2048,8,48]{0,1,2:T(8,128)(2,1)} async-done(((bf16[2048,8,12]{0,1,2:T(8,128)(2,1)}), bf16[2048,8,48]{0,1,2:T(8,128)(2,1)}) %all-gather.12.cloned.1.call-update) | async-done | bytes 1572880 | tf_op jit(solution)/shard_map/all_gather | solution.py:13
  168.8 8.1 fusion.104
  176.9 5.4 copy.66
  182.4 59.7 %reduce-scatter.12.cloned.1.call-done = f32[2048,8,12]{0,1,2:T(8,128)} async-done(((f32[2048,8,48]{0,1,2:T(8,128)}), f32[2048,8,12]{0,1,2:T(8,128)}) %reduce-scatter.12.cloned.1.call-update) | async-done | bytes 786448 | tf_op jit(solution)/shard_map/reduce_scatter | solution.py:16
  243.3 6.4 fusion.171
  250.9 36.3 %all-gather.14.cloned.1.call-done = bf16[2048,8,48]{0,1,2:T(8,128)(2,1)} async-done(((bf16[2048,8,12]{0,1,2:T(8,128)(2,1)}), bf16[2048,8,48]{0,1,2:T(8,128)(2,1)}) %all-gather.14.cloned.1.call-update) | async-done | bytes 1572880 | tf_op jit(solution)/shard_map/all_gather | solution.py:13
  287.2 8.1 fusion.102
  295.3 5.4 copy.70
  300.8 59.7 %reduce-scatter.14.cloned.1.call-done = f32[2048,8,12]{0,1,2:T(8,128)} async-done(((f32[2048,8,48]{0,1,2:T(8,128)}), f32[2048,8,12]{0,1,2:T(8,128)}) %reduce-scatter.14.cloned.1.call-update) | async-done | bytes 786448 | tf_op jit(solution)/shard_map/reduce_scatter | solution.py:16
  366.7 9.9 reshape.165
  376.6 14.6 all_to_all.216
  394.5 12.5 reshape.166
  426.5 17.8 all-to-all-done.1
  466.2 6.0 select_reduce_fusion.2
  567.9 5.9 fusion.258
  576.7 21.8 %all_to_all.217 = f32[128,32,48]{0,1,2:T(8,128)S(1)} all-to-all(f32[128,32,48]{0,1,2:T(8,128)S(1)} %copy.84), channel_id=1, replica_groups=mesh['case'=2,'model'=4,'ens'=4] {'model'}, dimensions={2} | all-to-all | bytes 1572864 | tf_op jit(solution)/shard_map/all_to_all | solution.py:54
  599.4 16.9 all_to_all.218
  616.7 6.3 fusion.168
  624.1 35.3 %all-gather.16.cloned.1.call-done = bf16[2048,8,48]{0,1,2:T(8,128)(2,1)} async-done(((bf16[2048,8,12]{0,1,2:T(8,128)(2,1)}), bf16[2048,8,48]{0,1,2:T(8,128)(2,1)}) %all-gather.16.cloned.1.call-update) | async-done | bytes 1572880 | tf_op jit(solution)/shard_map/all_gather | solution.py:13
  659.4 8.3 fusion.100
  667.7 5.4 copy.91
  673.1 59.7 %reduce-scatter.16.cloned.1.call-done = f32[2048,8,12]{0,1,2:T(8,128)} async-done(((f32[2048,8,48]{0,1,2:T(8,128)}), f32[2048,8,12]{0,1,2:T(8,128)}) %reduce-scatter.16.cloned.1.call-update) | async-done | bytes 786448 | tf_op jit(solution)/shard_map/reduce_scatter | solution.py:16
  734.9 6.4 fusion.165
  742.5 36.3 %all-gather.18.cloned.1.call-done = bf16[2048,8,48]{0,1,2:T(8,128)(2,1)} async-done(((bf16[2048,8,12]{0,1,2:T(8,128)(2,1)}), bf16[2048,8,48]{0,1,2:T(8,128)(2,1)}) %all-gather.18.cloned.1.call-update) | async-done | bytes 1572880 | tf_op jit(solution)/shard_map/all_gather | solution.py:13
  778.8 7.2 fusion.98
  789.6 59.7 %reduce-scatter.18.cloned.1.call-done = f32[2048,8,12]{0,1,2:T(8,128)} async-done(((f32[2048,8,48]{0,1,2:T(8,128)}), f32[2048,8,12]{0,1,2:T(8,128)}) %reduce-scatter.18.cloned.1.call-update) | async-done | bytes 786448 | tf_op jit(solution)/shard_map/reduce_scatter | solution.py:16
  851.4 6.4 fusion.162
  859.2 36.1 %all-gather.20.cloned.1.call-done = bf16[2048,8,48]{0,1,2:T(8,128)(2,1)} async-done(((bf16[2048,8,12]{0,1,2:T(8,128)(2,1)}), bf16[2048,8,48]{0,1,2:T(8,128)(2,1)}) %all-gather.20.cloned.1.call-update) | async-done | bytes 1572880 | tf_op jit(solution)/shard_map/all_gather | solution.py:13
  895.3 7.2 fusion.96
  906.1 59.7 %reduce-scatter.20.cloned.1.call-done = f32[2048,8,12]{0,1,2:T(8,128)} async-done(((f32[2048,8,48]{0,1,2:T(8,128)}), f32[2048,8,12]{0,1,2:T(8,128)}) %reduce-scatter.20.cloned.1.call-update) | async-done | bytes 786448 | tf_op jit(solution)/shard_map/reduce_scatter | solution.py:16
  971.9 9.9 reshape.169
  981.8 14.3 all_to_all.219
  999.0 12.5 reshape.170
  1024.6 23.0 %all_to_all.220 = f32[4,1,49152]{2,1,0:T(1,128)S(1)} all-to-all(f32[4,1,49152]{2,1,0:T(1,128)S(1)} %reshape.171), channel_id=1, replica_groups=mesh['case'=2,'model'=4,'ens'=4] {'model'}, dimensions={0} | all-to-all | bytes 1572864 | tf_op jit(solution)/shard_map/all_to_all | solution.py:51
  1070.0 6.0 select_reduce_fusion.1
  1171.6 5.7 fusion.261
  1180.2 22.4 %all_to_all.221 = f32[128,32,48]{0,1,2:T(8,128)S(1)} all-to-all(f32[128,32,48]{0,1,2:T(8,128)S(1)} %copy.113), channel_id=1, replica_groups=mesh['case'=2,'model'=4,'ens'=4] {'model'}, dimensions={2} | all-to-all | bytes 1572864 | tf_op jit(solution)/shard_map/all_to_all | solution.py:54
  1203.5 17.3 all_to_all.222
  1221.3 6.3 fusion.159
  1228.7 34.2 %all-gather.22.cloned.1.call-done = bf16[2048,8,48]{0,1,2:T(8,128)(2,1)} async-done(((bf16[2048,8,12]{0,1,2:T(8,128)(2,1)}), bf16[2048,8,48]{0,1,2:T(8,128)(2,1)}) %all-gather.22.cloned.1.call-update) | async-done | bytes 1572880 | tf_op jit(solution)/shard_map/all_gather | solution.py:13
  1262.9 8.5 fusion.94
  1271.4 5.4 copy.120
  1276.9 59.7 %reduce-scatter.22.cloned.1.call-done = f32[2048,8,12]{0,1,2:T(8,128)} async-done(((f32[2048,8,48]{0,1,2:T(8,128)}), f32[2048,8,12]{0,1,2:T(8,128)}) %reduce-scatter.22.cloned.1.call-update) | async-done | bytes 786448 | tf_op jit(solution)/shard_map/reduce_scatter | solution.py:16
  1338.6 6.4 fusion.156
  1346.2 36.4 %all-gather.24.cloned.1.call-done = bf16[2048,8,48]{0,1,2:T(8,128)(2,1)} async-done(((bf16[2048,8,12]{0,1,2:T(8,128)(2,1)}), bf16[2048,8,48]{0,1,2:T(8,128)(2,1)}) %all-gather.24.cloned.1.call-update) | async-done | bytes 1572880 | tf_op jit(solution)/shard_map/all_gather | solution.py:13
  1382.6 7.2 fusion.92
  1393.3 59.7 %reduce-scatter.24.cloned.1.call-done = f32[2048,8,12]{0,1,2:T(8,128)} async-done(((f32[2048,8,48]{0,1,2:T(8,128)}), f32[2048,8,12]{0,1,2:T(8,128)}) %reduce-scatter.24.cloned.1.call-update) | async-done | bytes 786448 | tf_op jit(solution)/shard_map/reduce_scatter | solution.py:16
  1455.1 6.4 fusion.153
  1462.7 36.3 %all-gather.26.cloned.1.call-done = bf16[2048,8,48]{0,1,2:T(8,128)(2,1)} async-done(((bf16[2048,8,12]{0,1,2:T(8,128)(2,1)}), bf16[2048,8,48]{0,1,2:T(8,128)(2,1)}) %all-gather.26.cloned.1.call-update) | async-done | bytes 1572880 | tf_op jit(solution)/shard_map/all_gather | solution.py:13
  1499.0 7.2 fusion.90
  1509.8 59.7 %reduce-scatter.26.cloned.1.call-done = f32[2048,8,12]{0,1,2:T(8,128)} async-done(((f32[2048,8,48]{0,1,2:T(8,128)}), f32[2048,8,12]{0,1,2:T(8,128)}) %reduce-scatter.26.cloned.1.call-update) | async-done | bytes 786448 | tf_op jit(solution)/shard_map/reduce_scatter | solution.py:16
  1575.6 9.9 reshape.173
  1585.5 14.6 all_to_all.223
  1603.0 12.5 reshape.174
  1628.6 23.0 %all_to_all.224 = f32[4,1,49152]{2,1,0:T(1,128)S(1)} all-to-all(f32[4,1,49152]{2,1,0:T(1,128)S(1)} %reshape.175), channel_id=1, replica_groups=mesh['case'=2,'model'=4,'ens'=4] {'model'}, dimensions={0} | all-to-all | bytes 1572864 | tf_op jit(solution)/shard_map/all_to_all | solution.py:51
  1673.7 6.0 select_reduce_fusion
  1775.4 5.7 fusion.264
  1784.1 22.4 %all_to_all.225 = f32[128,32,48]{0,1,2:T(8,128)S(1)} all-to-all(f32[128,32,48]{0,1,2:T(8,128)S(1)} %copy.142), channel_id=1, replica_groups=mesh['case'=2,'model'=4,'ens'=4] {'model'}, dimensions={2} | all-to-all | bytes 1572864 | tf_op jit(solution)/shard_map/all_to_all | solution.py:54
  1807.3 17.3 all_to_all.226
  (349 shorter events, 478.8 us)
Async XLA Ops:
  6.5 46.6 %all-gather.10.cloned.1.call-start = ((), (), s32[]{:S(2)}) async-start(), calls=%async_computation.21 | async-start | bytes 1966080 | tf_op jit(solution)/shard_map/all_gather | solution.py:13
  7.7 45.5 %copy-start.35 = (bf16[3,192,48]{1,2,0:T(8,128)(2,1)S(1)}, bf16[3,192,48]{1,2,0:T(8,128)(2,1)}, u32[]{:S(2)}) copy-start(bf16[3,192,48]{1,2,0:T(8,128)(2,1)} %param.15) | copy-start | bytes 165892
  7.7 45.4 %copy-start.38 = (bf16[3,48,192]{2,1,0:T(8,128)(2,1)S(1)}, bf16[3,48,192]{2,1,0:T(8,128)(2,1)}, u32[]{:S(2)}) copy-start(bf16[3,48,192]{2,1,0:T(8,128)(2,1)} %param.14) | copy-start | bytes 165892
  15.1 108.5 %reduce-scatter.10.cloned.1.call-start = ((), (), s32[]{:S(2)}) async-start(), calls=%async_computation.22 | async-start | bytes 3932160 | tf_op jit(solution)/shard_map/reduce_scatter | solution.py:16
  63.9 59.7 %copy-start = (f32[8,2048,12]{1,0,2:T(8,128)S(1)}, f32[8,2048,12]{1,0,2:T(8,128)}, u32[]{:S(2)}) copy-start(f32[8,2048,12]{1,0,2:T(8,128)} %param.12) | copy-start | bytes 2359300
  63.9 104.8 %all-gather.12.cloned.1.call-start = ((), (), s32[]{:S(2)}) async-start(), calls=%async_computation.23 | async-start | bytes 1966080 | tf_op jit(solution)/shard_map/all_gather | solution.py:13
  132.2 109.8 %reduce-scatter.12.cloned.1.call-start = ((), (), s32[]{:S(2)}) async-start(), calls=%async_computation.24 | async-start | bytes 3932160 | tf_op jit(solution)/shard_map/reduce_scatter | solution.py:16
  182.3 59.7 %copy-start.4 = (f32[2048,8,12]{0,1,2:T(8,128)S(1)}, f32[2048,8,12]{0,1,2:T(8,128)}, u32[]{:S(2)}) copy-start(f32[2048,8,12]{0,1,2:T(8,128)} %reduce-scatter.10.cloned.1.call-done) | copy-start | bytes 2359300
  182.3 104.9 %all-gather.14.cloned.1.call-start = ((), (), s32[]{:S(2)}) async-start(), calls=%async_computation.25 | async-start | bytes 1966080 | tf_op jit(solution)/shard_map/all_gather | solution.py:13
  250.7 109.8 %reduce-scatter.14.cloned.1.call-start = ((), (), s32[]{:S(2)}) async-start(), calls=%async_computation.26 | async-start | bytes 3932160 | tf_op jit(solution)/shard_map/reduce_scatter | solution.py:16
  300.7 59.7 %copy-start.9 = (f32[2048,8,12]{0,1,2:T(8,128)S(1)}, f32[2048,8,12]{0,1,2:T(8,128)}, u32[]{:S(2)}) copy-start(f32[2048,8,12]{0,1,2:T(8,128)} %reduce-scatter.12.cloned.1.call-done) | copy-start | bytes 2359300
  416.3 9.6 copy-start.41
  421.1 23.3 %all-to-all-start.1 = ((f32[4,1,49152]{2,1,0:T(1,128)}), f32[4,1,49152]{2,1,0:T(1,128)S(1)}, u32[]{:S(2)}, u32[]{:S(2)}) async-start(f32[4,1,49152]{2,1,0:T(1,128)} %reshape.167), calls=%async_computation.4 | async-start | bytes 1572864 | tf_op jit(solution)/shard_map/all_to_all | solution.py:51
  424.6 234.8 %all-gather.16.cloned.1.call-start = ((), (), s32[]{:S(2)}) async-start(), calls=%async_computation.27 | async-start | bytes 1966080 | tf_op jit(solution)/shard_map/all_gather | solution.py:13
  425.9 36.0 %copy-start.34 = (s32[1024]{0:T(1024)}, s32[1024]{0:T(1024)S(1)}, u32[]{:S(2)}) copy-start(s32[1024]{0:T(1024)S(1)} %pad_clamp_fusion) | copy-start | bytes 12292
  426.5 35.9 %copy-start.28 = (pred[12]{0:T(512)(128)(4,1)}, pred[12]{0:T(512)(128)(4,1)S(1)}, u32[]{:S(2)}) copy-start(pred[12]{0:T(512)(128)(4,1)S(1)} %compare_and_fusion) | copy-start | bytes 40
  454.1 3.2 copy-start.15
  461.9 0.7 copy-start.22
  463.4 2.9 copy-start.19
  463.4 2.9 copy-start.25
  548.4 3.6 copy-start.11
  548.4 3.6 copy-start.29
  554.1 4.5 copy-start.2
  561.2 6.7 copy-start.16
  616.7 42.7 %copy-start.36 = (bf16[3,192,48]{1,2,0:T(8,128)(2,1)S(1)}, bf16[3,192,48]{1,2,0:T(8,128)(2,1)}, u32[]{:S(2)}) copy-start(bf16[3,192,48]{1,2,0:T(8,128)(2,1)} %param.15) | copy-start | bytes 165892
  616.7 42.7 %copy-start.39 = (bf16[3,48,192]{2,1,0:T(8,128)(2,1)S(1)}, bf16[3,48,192]{2,1,0:T(8,128)(2,1)}, u32[]{:S(2)}) copy-start(bf16[3,48,192]{2,1,0:T(8,128)(2,1)} %param.14) | copy-start | bytes 165892
  624.0 108.8 %reduce-scatter.16.cloned.1.call-start = ((), (), s32[]{:S(2)}) async-start(), calls=%async_computation.28 | async-start | bytes 3932160 | tf_op jit(solution)/shard_map/reduce_scatter | solution.py:16
  673.1 105.7 %all-gather.18.cloned.1.call-start = ((), (), s32[]{:S(2)}) async-start(), calls=%async_computation.29 | async-start | bytes 1966080 | tf_op jit(solution)/shard_map/all_gather | solution.py:13
  742.3 107.0 %reduce-scatter.18.cloned.1.call-start = ((), (), s32[]{:S(2)}) async-start(), calls=%async_computation.30 | async-start | bytes 3932160 | tf_op jit(solution)/shard_map/reduce_scatter | solution.py:16
  789.6 59.7 %copy-start.5 = (f32[2048,8,12]{0,1,2:T(8,128)S(1)}, f32[2048,8,12]{0,1,2:T(8,128)}, u32[]{:S(2)}) copy-start(f32[2048,8,12]{0,1,2:T(8,128)} %get-tuple-element.18) | copy-start | bytes 2359300
  789.6 105.7 %all-gather.20.cloned.1.call-start = ((), (), s32[]{:S(2)}) async-start(), calls=%async_computation.31 | async-start | bytes 1966080 | tf_op jit(solution)/shard_map/all_gather | solution.py:13
  858.8 107.0 %reduce-scatter.20.cloned.1.call-start = ((), (), s32[]{:S(2)}) async-start(), calls=%async_computation.32 | async-start | bytes 3932160 | tf_op jit(solution)/shard_map/reduce_scatter | solution.py:16
  906.0 59.7 %copy-start.7 = (f32[2048,8,12]{0,1,2:T(8,128)S(1)}, f32[2048,8,12]{0,1,2:T(8,128)}, u32[]{:S(2)}) copy-start(f32[2048,8,12]{0,1,2:T(8,128)} %get-tuple-element.16) | copy-start | bytes 2359300
  906.1 356.8 %all-gather.22.cloned.1.call-start = ((), (), s32[]{:S(2)}) async-start(), calls=%async_computation.33 | async-start | bytes 1966080 | tf_op jit(solution)/shard_map/all_gather | solution.py:13
  1058.8 2.0 copy-start.17
  1065.5 0.8 copy-start.23
  1065.5 0.8 copy-start.30
  1067.1 2.9 copy-start.20
  1067.1 2.9 copy-start.26
  1152.1 3.6 copy-start.12
  1152.1 3.6 copy-start.31
  1157.9 4.5 copy-start.3
  1164.9 6.7 copy-start.18
  1221.3 41.6 %copy-start.37 = (bf16[3,192,48]{1,2,0:T(8,128)(2,1)S(1)}, bf16[3,192,48]{1,2,0:T(8,128)(2,1)}, u32[]{:S(2)}) copy-start(bf16[3,192,48]{1,2,0:T(8,128)(2,1)} %param.15) | copy-start | bytes 165892
  1221.3 41.6 %copy-start.40 = (bf16[3,48,192]{2,1,0:T(8,128)(2,1)S(1)}, bf16[3,48,192]{2,1,0:T(8,128)(2,1)}, u32[]{:S(2)}) copy-start(bf16[3,48,192]{2,1,0:T(8,128)(2,1)} %param.14) | copy-start | bytes 165892
  1228.6 107.9 %reduce-scatter.22.cloned.1.call-start = ((), (), s32[]{:S(2)}) async-start(), calls=%async_computation.34 | async-start | bytes 3932160 | tf_op jit(solution)/shard_map/reduce_scatter | solution.py:16
  1276.8 105.7 %all-gather.24.cloned.1.call-start = ((), (), s32[]{:S(2)}) async-start(), calls=%async_computation.35 | async-start | bytes 1966080 | tf_op jit(solution)/shard_map/all_gather | solution.py:13
  1346.0 107.0 %reduce-scatter.24.cloned.1.call-start = ((), (), s32[]{:S(2)}) async-start(), calls=%async_computation.36 | async-start | bytes 3932160 | tf_op jit(solution)/shard_map/reduce_scatter | solution.py:16
  1393.3 59.7 %copy-start.6 = (f32[2048,8,12]{0,1,2:T(8,128)S(1)}, f32[2048,8,12]{0,1,2:T(8,128)}, u32[]{:S(2)}) copy-start(f32[2048,8,12]{0,1,2:T(8,128)} %get-tuple-element.12) | copy-start | bytes 2359300
  1393.3 105.8 %all-gather.26.cloned.1.call-start = ((), (), s32[]{:S(2)}) async-start(), calls=%async_computation.37 | async-start | bytes 1966080 | tf_op jit(solution)/shard_map/all_gather | solution.py:13
  1462.5 107.0 %reduce-scatter.26.cloned.1.call-start = ((), (), s32[]{:S(2)}) async-start(), calls=%async_computation.38 | async-start | bytes 3932160 | tf_op jit(solution)/shard_map/reduce_scatter | solution.py:16
  1509.8 59.7 %copy-start.8 = (f32[2048,8,12]{0,1,2:T(8,128)S(1)}, f32[2048,8,12]{0,1,2:T(8,128)}, u32[]{:S(2)}) copy-start(f32[2048,8,12]{0,1,2:T(8,128)} %get-tuple-element.10) | copy-start | bytes 2359300
  1662.6 2.0 copy-start.13
  1669.2 0.8 copy-start.24
  1669.3 0.8 copy-start.32
  1670.9 2.9 copy-start.21
  1670.9 2.9 copy-start.27
  1755.9 3.6 copy-start.10
  1755.9 3.6 copy-start.33
  1761.7 4.5 copy-start.1
  1768.7 6.7 copy-start.14
Sparse Core Ops, SparseCore 0:
  15.3 37.8 all-gather.9
  64.1 59.5 reduce-scatter.9
  132.3 36.4 all-gather.11
  182.5 59.5 reduce-scatter.11
  250.8 36.4 all-gather.13
  300.9 59.5 reduce-scatter.13
  624.2 35.1 all-gather.15
  673.2 59.5 reduce-scatter.15
  742.4 36.4 all-gather.17
  789.7 59.5 reduce-scatter.17
  858.9 36.4 all-gather.19
  906.2 59.5 reduce-scatter.19
  1228.7 34.0 all-gather.21
  1276.9 59.5 reduce-scatter.21
  1346.1 36.4 all-gather.23
  1393.4 59.5 reduce-scatter.23
  1462.6 36.4 all-gather.25
  1509.9 59.5 reduce-scatter.25
where the time goes:
time: 1840 us; the launch traced here: 1830 us
  waiting for transfers between devices  880 us (48%)
  matrix products  445 us (24%)
  local copies, waits for them, and re-layouts  234 us (13%)
  blocking collectives  208 us (11%)
  other arithmetic  44 us (2%)
    reduce_scatter x9, waiting for transfers between devices, value_a8(): lax.psum_scatter(part_sum, 'model', scatter_dimension=2, tiled=True)  537 us
    all_gather x9, waiting for transfers between devices, value_a8(): mix_full = lax.all_gather(mix_out, 'model', axis=2, tiled=True)  325 us
    unnamed x96, local copies, waits for them, and re-layouts  90.4 us
    dot_general x33, matrix products, letkf_weights(): t_mat = 1.5 * identity - 0.5 * jnp.matmul(z_mat, b_mat, precision=FULL_PREC)  87.9 us
    dot_general x33, matrix products, letkf_weights(): z_mat = jnp.matmul(t_mat, z_mat, precision=FULL_PREC)  87.1 us
    dot_general x33, matrix products, letkf_weights(): b_mat = jnp.matmul(b_mat, t_mat, precision=FULL_PREC)  84.7 us
    dot_general x9, matrix products, value_a8(): jnp.einsum('ikf,fv->ikv', hidden.astype(jnp.bfloat16), w_out[layer_idx],...  69.2 us
    all_to_all x3, blocking collectives, local_step(): col_state = lax.all_to_all(col_state, 'model', 2, 0, tiled=True)  66.7 us
  transfers between devices with their start and end apart: 19, of which 19 were waited for; matrix products, arithmetic and copies ran while one was open for 0% of the time, Pallas kernels for 0%

commit v1 on v0

v1 whole, which is shorter than its diff:
```python
import functools

import jax
import jax.numpy as jnp
from jax import lax
from jax.experimental import pallas as pl
from jax.experimental.pallas import tpu as pltpu
from jax.sharding import PartitionSpec as P

NS_STEPS = 12
MESH_IDS = pl.DeviceIdType.MESH
F32 = jnp.float32
BF16 = jnp.bfloat16
C1 = 0.7978845608028654
C2 = 0.7978845608028654 * 0.044715


def gelu(x):
    th = jnp.tanh(x * (C1 + C2 * (x * x)))
    half = 0.5 * x
    return half + half * th


def kernel(dims, idx_ref, rho_ref, x0_ref, a_hbm, wu_ref, y_ref, r_ref, out_ref,
           a_v, at, wu_all, wt, ut, s0, r0, hw, hb, mt, recv_c, recv_f, send_f, out_s, out_r,
           v_s, f_s, ft_s, m_s, c_m, dn_m, dz_m, t_m, q_m,
           sem_a, sem_ws, sem_wr, sem_is, sem_ir, sem_cs, sem_cr, sem_fs, sem_fr, sem_os, sem_or):
    cycles, layers, n_obs = dims
    me_e = lax.axis_index("ens")
    me_m = lax.axis_index("model")
    me = me_e * 4 + me_m
    my_half = me_m // 2
    members = 32

    def ids(te, tm):
        return {"ens": te, "model": tm}

    bar = pltpu.get_barrier_semaphore()
    for de in range(4):
        for dm in range(4):
            if (de, dm) != (0, 0):
                pl.semaphore_signal(bar, inc=1, device_id=ids((me_e + de) % 4, (me_m + dm) % 4), device_id_type=MESH_IDS)
    copy_a = pltpu.make_async_copy(a_hbm, a_v, sem_a)
    copy_a.start()

    for j in range(16):
        out_s[j] = x0_ref[:, j * 128:(j + 1) * 128]
        for a in range(2):
            for d in range(4):
                s0[a, d, :, j * 128:(j + 1) * 128] = out_s[j, pl.ds(2 * d + a, 12, stride=8), :]
    pl.semaphore_wait(bar, 15)

    def init_copy(a, dm):
        tm = (me_m + dm) % 4
        return pltpu.make_async_remote_copy(
            src_ref=s0.at[a, tm], dst_ref=r0.at[a, me_m], send_sem=sem_is.at[a, tm], recv_sem=sem_ir.at[a, me_m],
            device_id=ids(me_e, tm), device_id_type=MESH_IDS)

    def init_wait(a, dm):
        tm = (me_m + dm) % 4
        return pltpu.make_async_remote_copy(
            src_ref=s0.at[a, tm], dst_ref=r0.at[a, tm], send_sem=sem_is.at[a, tm], recv_sem=sem_ir.at[a, tm],
            device_id=ids(me_e, tm), device_id_type=MESH_IDS)

    def w_copy(dm):
        tm = (me_m + dm) % 4
        return pltpu.make_async_remote_copy(
            src_ref=wu_ref, dst_ref=wu_all.at[me_m], send_sem=sem_ws.at[tm], recv_sem=sem_wr.at[me_m],
            device_id=ids(me_e, tm), device_id_type=MESH_IDS)

    def w_wait(dm):
        tm = (me_m + dm) % 4
        return pltpu.make_async_remote_copy(
            src_ref=wu_ref, dst_ref=wu_all.at[tm], send_sem=sem_ws.at[tm], recv_sem=sem_wr.at[tm],
            device_id=ids(me_e, tm), device_id_type=MESH_IDS)

    for dm in (2, 1, 3):
        init_copy(0, dm).start()
    for dm in (2, 1, 3):
        w_copy(dm).start()
    for dm in (2, 1, 3):
        init_copy(1, dm).start()
    for a in range(2):
        r0[a, me_m] = s0[a, me_m]
    wu_all[me_m] = wu_ref[...]
    mt[48:128, :] = jnp.zeros((80, 2048), BF16)

    copy_a.wait()
    row = lax.broadcasted_iota(jnp.int32, (256, 256), 0)
    col = lax.broadcasted_iota(jnp.int32, (256, 256), 1)
    eye = jnp.where(row == col, 1.0, 0.0).astype(BF16)

    def flip(i, carry):
        for j in range(8):
            tile = a_v[pl.ds(pl.multiple_of(i * 256, 256), 256), j * 256:(j + 1) * 256]
            at[j * 256:(j + 1) * 256, pl.ds(pl.multiple_of(i * 256, 256), 256)] = lax.dot_general(
                eye, tile, (((1,), (1,)), ((), ())), preferred_element_type=F32).astype(BF16)
        return carry

    lax.fori_loop(0, 8, flip, 0)

    for dm in (2, 1, 3):
        w_wait(dm).wait()
    lane = lax.broadcasted_iota(jnp.int32, (192, 128), 1)
    for l in range(layers):
        parts = []
        for q in range(4):
            piece = wu_all[q, l].astype(F32)
            wt[l, q * 192:(q + 1) * 192, :] = jnp.where(lane < 48, piece, 0.0).astype(BF16)
            parts.append(piece)
        ut[l] = jnp.transpose(jnp.concatenate(parts, axis=0))[64:112, :].astype(BF16)

    def pick(i):
        half = (my_half + 1 - i // 8) % 2
        te = (me_e + (i % 8) // 2) % 4
        tm = 2 * half + i % 2
        return te, tm, te * 4 + tm

    def c_copy(a, te, tm, slot):
        t = te * 4 + tm
        return pltpu.make_async_remote_copy(
            src_ref=hw.at[a, :, pl.ds(pl.multiple_of(t * 128, 128), 128)], dst_ref=recv_c.at[slot, a],
            send_sem=sem_cs.at[a, t], recv_sem=sem_cr.at[a, slot], device_id=ids(te, tm), device_id_type=MESH_IDS)

    def f_copy(a, te, tm, slot):
        t = te * 4 + tm
        return pltpu.make_async_remote_copy(
            src_ref=send_f.at[a, t], dst_ref=recv_f.at[a, slot],
            send_sem=sem_fs.at[a, t], recv_sem=sem_fr.at[a, slot], device_id=ids(te, tm), device_id_type=MESH_IDS)

    def o_copy(te, tm, slot):
        t = te * 4 + tm
        return pltpu.make_async_remote_copy(
            src_ref=out_s.at[t], dst_ref=out_r.at[:, pl.ds(pl.multiple_of(slot * 128, 128), 128)],
            send_sem=sem_os.at[t], recv_sem=sem_or.at[slot], device_id=ids(te, tm), device_id_type=MESH_IDS)

    def others(fn):
        def body(i, carry):
            te, tm, t = pick(i)

            @pl.when(t != me)
            def _():
                fn(te, tm, t)
            return carry
        lax.fori_loop(0, 16, body, 0)

    def forecast(cyc, a):
        @pl.when(cyc == 0)
        def _():
            for dm in (2, 1, 3):
                init_wait(a, dm).wait()
            for q in range(4):
                hw[a, q * 12:(q + 1) * 12, :] = r0[a, q]
            hb[...] = hw[a].astype(BF16)

        @pl.when(cyc > 0)
        def _():
            def drain(te, tm, t):
                c_copy(a, te, tm, t).wait_send()
                f_copy(a, te, tm, t).wait()
            others(drain)

            def load(j, carry):
                sl = pl.ds(pl.multiple_of(j * 128, 128), 128)
                block = recv_f[a, j]
                hw[a, :, sl] = block
                hb[:, sl] = block.astype(BF16)
                return carry
            lax.fori_loop(0, 16, load, 0)

        def layer(l, carry):
            for n in range(4):
                mt[0:48, n * 512:(n + 1) * 512] = jnp.dot(
                    hb[...], at[:, n * 512:(n + 1) * 512], preferred_element_type=F32).astype(BF16)

            def tile(i, inner):
                half = (my_half + 1 - i // 4) % 2
                te = (me_e + i % 4) % 4
                sl = pl.ds(pl.multiple_of((2 * te + half) * 256, 256), 256)
                mix = mt[:, sl]
                new = hw[a, :, sl]
                upd = None
                for n in range(3):
                    hid = jnp.dot(wt[l, n * 256:(n + 1) * 256, :], mix, preferred_element_type=F32)
                    part = jnp.dot(ut[l, :, n * 256:(n + 1) * 256], gelu(hid).astype(BF16), preferred_element_type=F32)
                    upd = part if upd is None else upd + part
                new = new + upd
                hw[a, :, sl] = new
                hb[:, sl] = new.astype(BF16)

                @pl.when(l == layers - 1)
                def _():
                    for b in range(2):
                        tm = 2 * half + b
                        t = te * 4 + tm

                        @pl.when(t != me)
                        def _():
                            c_copy(a, te, tm, me).start()

                        @pl.when(t == me)
                        def _():
                            recv_c[me, a] = new[:, b * 128:(b + 1) * 128]
                return inner
            lax.fori_loop(0, 8, tile, 0)
            return carry
        lax.fori_loop(0, layers, layer, 0)

    def mat(p_ref, rows):
        out = []
        for i in range(n_obs):
            acc = None
            for k in range(n_obs):
                term = p_ref[i, k:k + 1, :] * rows[k]
                acc = term if acc is None else acc + term
            out.append(acc)
        return out

    def vec(p_ref, x):
        acc = None
        for k in range(n_obs):
            term = x[k:k + 1, :] * p_ref[k]
            acc = term if acc is None else acc + term
        return acc

    sub = lax.broadcasted_iota(jnp.int32, (n_obs, 128), 0)
    units = [jnp.where(sub == i, 1.0, 0.0).astype(F32) for i in range(n_obs)]
    c0 = (members - 1) / rho_ref[0]

    def analyse(cyc):
        for a in range(2):
            others(lambda te, tm, t: c_copy(a, te, tm, t).wait_recv())

        def add(j, acc):
            return acc + (recv_c[j, 0] + recv_c[j, 1])
        mean = lax.fori_loop(0, 16, add, jnp.zeros((48, 128), F32)) * (1.0 / members)
        m_s[...] = mean

        def centre(j, carry):
            for a in range(2):
                recv_c[j, a] = recv_c[j, a] - mean
            return carry
        lax.fori_loop(0, 16, centre, 0)

        root = jnp.sqrt(r_ref[...])
        for p in range(n_obs):
            ip = idx_ref[p]
            v_s[:, :, p:p + 1, :] = recv_c[:, :, pl.ds(ip, 1), :] * root[p:p + 1, :]

        for grp in range(0, n_obs, 6):
            def outer(j, accs):
                accs = list(accs)
                for a in range(2):
                    x = recv_c[j, a]
                    for p in range(6):
                        accs[p] = accs[p] + v_s[j, a, grp + p:grp + p + 1, :] * x
                return tuple(accs)
            sums = lax.fori_loop(0, 16, outer, tuple(jnp.zeros((48, 128), F32) for _ in range(6)))
            for p in range(6):
                f_s[grp + p] = sums[p]

        gain = []
        for q in range(n_obs):
            iq = idx_ref[q]
            c_m[:, q:q + 1, :] = f_s[:, pl.ds(iq, 1), :] * root[q:q + 1, :]
            gain.append(root[q:q + 1, :] * (y_ref[cyc, q:q + 1, :] - m_s[pl.ds(iq, 1), :]))
        gain = jnp.concatenate(gain, axis=0)

        trace = None
        for p in range(n_obs):
            term = c_m[p, p:p + 1, :]
            trace = term if trace is None else trace + term
        trace = trace + members * c0
        inv = 1.0 / trace
        for p in range(n_obs):
            dn_m[p] = units[p] * inv
            dz_m[p] = jnp.zeros((n_obs, 128), F32)

        def step(i, carry):
            n, z = carry
            t = 1.5 - 0.5 * n
            c_rows = [c_m[k] for k in range(n_obs)]
            nc = mat(dn_m, c_rows)
            for p in range(n_obs):
                t_m[p] = t * units[p] - 0.5 * nc[p]
            tz = mat(t_m, [dz_m[k] for k in range(n_obs)])
            tt = mat(t_m, [t_m[k] for k in range(n_obs)])
            for p in range(n_obs):
                dz_m[p] = tz[p] - (0.5 * z) * dn_m[p]
                q_m[p] = tt[p] - (0.5 * n) * (t_m[p] + t * units[p])
            dn = mat(dn_m, [q_m[k] for k in range(n_obs)])
            for p in range(n_obs):
                dn_m[p] = dn[p]
            return n * t * t, t * z
        n, z = lax.fori_loop(0, NS_STEPS, step, (c0 * inv, jnp.ones((1, 128), F32)))

        rs = 1.0 / jnp.sqrt(trace)
        scale = float((members - 1) ** 0.5) * rs
        alpha = scale * z

        def apply_z(x):
            return z * x + vec(dz_m, vec(c_m, x))
        h = apply_z(apply_z(gain)) * inv

        base = m_s[...]
        for p in range(n_obs):
            base = base + h[p:p + 1, :] * f_s[p]
        m_s[...] = base
        for q in range(n_obs):
            acc = None
            for p in range(n_obs):
                term = (scale * dz_m[q, p:p + 1, :]) * f_s[p]
                acc = term if acc is None else acc + term
            ft_s[q] = acc

        def updated(t, a):
            acc = m_s[...] + alpha * recv_c[t, a]
            for q in range(n_obs):
                acc = acc + v_s[t, a, q:q + 1, :] * ft_s[q]
            return acc

        @pl.when(cyc < cycles - 1)
        def _():
            for a in range(2):
                def back(i, carry):
                    te, tm, t = pick(i)
                    new = updated(t, a)

                    @pl.when(t != me)
                    def _():
                        send_f[a, t] = new
                        f_copy(a, te, tm, me).start()

                    @pl.when(t == me)
                    def _():
                        recv_f[a, me] = new
                    return carry
                lax.fori_loop(0, 16, back, 0)

        @pl.when(cyc == cycles - 1)
        def _():
            def final(i, carry):
                te = (me_e + i) % 4
                for k in range(8):
                    new = updated(te * 4 + k // 2, k % 2)
                    for q in range(4):
                        out_s[te * 4 + q, pl.ds(k, 12, stride=8), :] = new[q * 12:(q + 1) * 12, :]
                for dm in (2, 1, 3, 0):
                    tm = (me_m + dm) % 4
                    t = te * 4 + tm

                    @pl.when(t != me)
                    def _():
                        o_copy(te, tm, me).start()

                    @pl.when(t == me)
                    def _():
                        out_r[:, pl.ds(pl.multiple_of(me * 128, 128), 128)] = out_s[me]
                return carry
            lax.fori_loop(0, 4, final, 0)

    def cycle(cyc, carry):
        forecast(cyc, 0)
        forecast(cyc, 1)
        analyse(cyc)
        return carry
    lax.fori_loop(0, cycles, cycle, 0)

    def finish(te, tm, t):
        for a in range(2):
            c_copy(a, te, tm, t).wait_send()
        o_copy(te, tm, t).wait()
    others(finish)
    out_ref[...] = out_r[...]


def solution(mesh):
    def local_step(ens_local, mix_op, w_in, w_out, obs_val, obs_prec, obs_idx, inflation):
        cycles, layers = obs_val.shape[0], w_in.shape[0]
        n_obs = obs_idx.shape[0]
        x0 = jnp.transpose(ens_local, (2, 0, 1)).reshape(96, 2048)
        zero = jnp.zeros((layers, 192, 16), BF16)
        wu = jnp.concatenate([jnp.transpose(w_in, (0, 2, 1)), zero, w_out, zero], axis=2)
        yobs = jnp.transpose(obs_val, (0, 2, 1))
        rinv = jnp.transpose(obs_prec)
        vmem = pl.BlockSpec(memory_space=pltpu.VMEM)
        smem = pl.BlockSpec(memory_space=pltpu.SMEM)
        dma = pltpu.SemaphoreType.DMA
        out = pl.pallas_call(
            functools.partial(kernel, (cycles, layers, n_obs)),
            out_shape=jax.ShapeDtypeStruct((96, 2048), F32),
            in_specs=[smem, smem, vmem, pl.BlockSpec(memory_space=pl.ANY), vmem, vmem, vmem],
            out_specs=vmem,
            scratch_shapes=[
                pltpu.VMEM((2048, 2048), BF16),
                pltpu.VMEM((2048, 2048), BF16),
                pltpu.VMEM((4, layers, 192, 128), BF16),
                pltpu.VMEM((layers, 768, 128), BF16),
                pltpu.VMEM((layers, 48, 768), BF16),
                pltpu.VMEM((2, 4, 12, 2048), F32),
                pltpu.VMEM((2, 4, 12, 2048), F32),
                pltpu.VMEM((2, 48, 2048), F32),
                pltpu.VMEM((48, 2048), BF16),
                pltpu.VMEM((128, 2048), BF16),
                pltpu.VMEM((16, 2, 48, 128), F32),
                pltpu.VMEM((2, 16, 48, 128), F32),
                pltpu.VMEM((2, 16, 48, 128), F32),
                pltpu.VMEM((16, 96, 128), F32),
                pltpu.VMEM((96, 2048), F32),
                pltpu.VMEM((16, 2, n_obs, 128), F32),
                pltpu.VMEM((n_obs, 48, 128), F32),
                pltpu.VMEM((n_obs, 48, 128), F32),
                pltpu.VMEM((48, 128), F32),
                pltpu.VMEM((n_obs, n_obs, 128), F32),
                pltpu.VMEM((n_obs, n_obs, 128), F32),
                pltpu.VMEM((n_obs, n_obs, 128), F32),
                pltpu.VMEM((n_obs, n_obs, 128), F32),
                pltpu.VMEM((n_obs, n_obs, 128), F32),
                dma(()),
                dma((4,)), dma((4,)),
                dma((2, 4)), dma((2, 4)),
                dma((2, 16)), dma((2, 16)),
                dma((2, 16)), dma((2, 16)),
                dma((16,)), dma((16,)),
            ],
            compiler_params=pltpu.CompilerParams(
                collective_id=0, has_side_effects=True, vmem_limit_bytes=60 * 1024 * 1024),
        )(obs_idx, inflation, x0, mix_op, wu, yobs, rinv)
        return jnp.transpose(out.reshape(12, 8, 2048), (1, 2, 0))

    member_spec = P(("case", "ens"), None, "model")
    col_axes = ("case", "ens", "model")
    in_specs = (member_spec, P(None, None), P(None, None, "model"), P(None, "model", None), P(None, col_axes, None), P(col_axes, None), P(None), P(None))
    return jax.shard_map(local_step, mesh=mesh, in_specs=in_specs, out_specs=member_spec, check_vma=False)
```

time: 1840 us -> 235 us (0.13)
  waiting for transfers between devices: 880 us -> 0 us
  matrix products: 445 us -> 0 us
  local copies, waits for them, and re-layouts: 234 us -> 4.18 us
  Pallas kernels: 0 us -> 228 us
  blocking collectives: 208 us -> 0 us
  other arithmetic: 44 us -> 0.85 us
    reduce_scatter x9 -> x0, waiting for transfers between devices: 537 us -> none  [value_a8(): lax.psum_scatter(part_sum, 'model', scatter_dimension=2, tiled=True)]
    dot_general x132 -> x0, matrix products: 445 us -> none  [the longest x33 87.9 us: letkf_weights(): t_mat = 1.5 * identity - 0.5 * jnp.matmul(z_mat, b_mat, precision=FULL_PREC)]
    all_gather x9 -> x0, waiting for transfers between devices: 325 us -> none  [value_a8(): mix_full = lax.all_gather(mix_out, 'model', axis=2, tiled=True)]
    pallas_call x0 -> x1, Pallas kernels: none -> 228 us  [local_step(): pl.pallas_call(functools.partial(kernel, (cycles, layers, n_obs)), out_sh...]
    all_to_all x11 -> x0, blocking collectives: 208 us -> none  [the longest x3 66.7 us: local_step(): col_state = lax.all_to_all(col_state, 'model', 2, 0, tiled=True)]
    unnamed x96 -> x3, local copies, waits for them, and re-layouts: 90.4 us -> 4.16 us
    all_to_all x28 -> x0, local copies, waits for them, and re-layouts: 48.7 us -> none  [the longest x10 28.4 us: local_step(): col_state = lax.all_to_all(ens_state, 'ens', 0, 1, tiled=True)]
    dot_general x9 -> x0, local copies, waits for them, and re-layouts: 38.9 us -> none  [value_a8(): jnp.einsum('ikf,fv->ikv', hidden.astype(jnp.bfloat16), w_out[layer_idx],...]
  transfers between devices with their start and end apart: 19 -> 0, of which waited for: 19 -> 0; matrix products, arithmetic and copies ran while one was open for 0% -> 0% of each run, Pallas kernels for 0% -> 0%
where the time goes in v1:
time: 235 us; the launch traced here: 233 us
  Pallas kernels  228 us (97%)
  local copies, waits for them, and re-layouts  4.18 us (2%)
    pallas_call x1, Pallas kernels, local_step(): pl.pallas_call(functools.partial(kernel, (cycles, layers, n_obs)), out_sh...  228 us

profile of v1, /device:TPU:2, one launch (start us, length us, event | category | flops | bytes accessed | tf_op | source)
XLA Modules:
  0.0 233.3 jit_solution(13264979185823176389)
XLA Ops:
  0.7 1.0 copy.9
  1.7 1.1 copy.10
  2.8 0.9 pad_maximum_fusion.wu_ref
  3.6 227.6 %shard_map.82 = f32[96,2048]{1,0:T(8,128)} custom-call(s32[12]{0:T(128)} %idx_ref.1, f32[1]{0:T(128)S(6)} %copy.12.rho_ref, f32[96,2048]{1,0:T(8,128)} %bitcast.10, bf16[2048,2048]{1,0:T(8,128)(2,1)} %a_hbm.1, bf16[3,192,128]{2,1,0:T(8,128)(2,1)} %pad_maximum_fusion.wu_ref, f32[3,12,128]{2,1,0:T(8,128)} %bitcast.12, f32[12,128]{1,0:T(8,128)} %bitcast.13), custom_call_target="tpu_custom_call" | custom-call | tf_op jit(solution)/shard_map/pallas_call | solution.py:389
  231.2 2.1 copy.13
  (1 shorter events, 0.0 us)

commit v2 on v1

v2 whole, which is shorter than its diff:
```python
import functools

import jax
import jax.numpy as jnp
from jax import lax
from jax.experimental import pallas as pl
from jax.experimental.pallas import tpu as pltpu
from jax.sharding import PartitionSpec as P

NS_STEPS = 12
MESH_IDS = pl.DeviceIdType.MESH
F32 = jnp.float32
BF16 = jnp.bfloat16
C1 = 0.7978845608028654
C2 = 0.7978845608028654 * 0.044715


def gelu(x):
    th = jnp.tanh(x * (C1 + C2 * (x * x)))
    half = 0.5 * x
    return half + half * th


def kernel(dims, idx_ref, rho_ref, x0_ref, a_hbm, w_ref, u_ref, y_in, r_in, out_ref,
           a_v, at, wall, wt, ut, s0, r0, relay, y_ref, r_ref, hw, hb, recv_c, recv_f, send_f, out_s, out_r,
           v_s, f_s, ft_s, m_s, c_m, dn_m, dz_m, t_m, q_m,
           sem_a, sem_ws, sem_wr, sem_ds, sem_dr, sem_bs, sem_br, sem_is, sem_ir, sem_rs, sem_rr,
           sem_cs, sem_cr, sem_fs, sem_fr, sem_os, sem_or):
    cycles, layers, n_obs = dims
    me_x = lax.axis_index("case")
    me_e = lax.axis_index("ens")
    me_z = lax.axis_index("model")
    grp = me_z // 2
    low = me_z % 2
    core = me_e % 2
    far = 1 - me_x
    mate = me_e + 1 - 2 * core
    me = me_e * 4 + me_x * 2 + low
    inside = grp == me_x
    members = 32

    def ids(tx, te, tz):
        return {"case": tx, "ens": te, "model": tz}

    def send(src, dst, ssem, rsem, dev):
        return pltpu.make_async_remote_copy(
            src_ref=src, dst_ref=dst, send_sem=ssem, recv_sem=rsem, device_id=dev, device_id_type=MESH_IDS)

    bar = pltpu.get_barrier_semaphore()
    for dx in range(2):
        for de in range(4):
            for dz in range(4):
                if (dx, de, dz) != (0, 0, 0):
                    pl.semaphore_signal(bar, inc=1, device_id=ids((me_x + dx) % 2, (me_e + de) % 4, (me_z + dz) % 4), device_id_type=MESH_IDS)
    copy_a = pltpu.make_async_copy(a_hbm, a_v, sem_a)
    copy_a.start()
    for j in range(16):
        out_s[j] = x0_ref[:, j * 128:(j + 1) * 128]
        for a in range(2):
            for i in range(4):
                s0[a, i, :, j * 128:(j + 1) * 128] = out_s[j, pl.ds(2 * i + a, 12, stride=8), :]
    wall[me_z, 0] = w_ref[...]
    wall[me_z, 1] = u_ref[...]
    pl.semaphore_wait(bar, 31)

    def i_copy(a, i):
        return send(s0.at[a, i], r0.at[a, me_z], sem_is.at[a, i], sem_ir.at[a, me_z], ids(i // 2, me_e, 2 * me_x + i % 2))

    def i_arrive(a, m):
        return send(s0.at[a, 0], r0.at[a, m], sem_is.at[a, 0], sem_ir.at[a, m], ids(far, me_e, me_z))

    def x_copy(a, k):
        i = 2 * far + k
        return send(s0.at[a, i], relay.at[a, k], sem_is.at[a, i], sem_rr.at[a, k], ids(far, me_e, me_z))

    def r_copy(a, k):
        return send(relay.at[a, k], r0.at[a, me_z], sem_rs.at[a, k], sem_ir.at[a, me_z], ids(me_x, me_e, 2 * far + k))

    def b_copy(n):
        dev = ids(me_z // 2, me_e, 2 * me_x + low)
        return send(y_in, y_ref, sem_bs.at[0], sem_br.at[0], dev) if n == 0 else send(r_in, r_ref, sem_bs.at[1], sem_br.at[1], dev)

    def w_copy(dz, slot):
        tz = (me_z + dz) % 4
        return send(wall.at[me_z, core], wall.at[slot, core], sem_ws.at[tz], sem_wr.at[slot], ids(me_x, me_e, tz))

    def d_copy(q, c):
        return send(wall.at[q, c], wall.at[q, c], sem_ds.at[q], sem_dr.at[q], ids(me_x, mate, me_z))

    def start_init(a):
        @pl.when(inside)
        def _():
            for i in range(4):
                @pl.when(me_z != i)
                def _():
                    i_copy(a, i).start()
            r0[a, me_z] = s0[a, me_z]

        @pl.when(jnp.logical_not(inside))
        def _():
            for k in range(2):
                x_copy(a, k).start()
            for k in range(2):
                i_copy(a, 2 * me_x + k).start()

    def start_relay(a):
        @pl.when(inside)
        def _():
            for k in range(2):
                x_copy(a, k).wait_recv()
                r_copy(a, k).start()

    def end_init(a):
        @pl.when(inside)
        def _():
            for i in range(4):
                @pl.when(me_z != i)
                def _():
                    i_copy(a, i).wait_send()
            for k in range(2):
                r_copy(a, k).wait_send()

        @pl.when(jnp.logical_not(inside))
        def _():
            for k in range(2):
                x_copy(a, k).wait_send()
                i_copy(a, 2 * me_x + k).wait_send()

    start_init(0)
    for dz in (2, 1, 3):
        w_copy(dz, me_z).start()
    start_relay(0)
    start_init(1)

    @pl.when(inside)
    def _():
        y_ref[...] = y_in[...]
        r_ref[...] = r_in[...]

    @pl.when(jnp.logical_not(inside))
    def _():
        b_copy(0).start()
        b_copy(1).start()
    start_relay(1)

    copy_a.wait()
    row = lax.broadcasted_iota(jnp.int32, (256, 256), 0)
    col = lax.broadcasted_iota(jnp.int32, (256, 256), 1)
    eye = jnp.where(row == col, 1.0, 0.0).astype(BF16)

    def flip(i, carry):
        for j in range(8):
            tile = a_v[pl.ds(pl.multiple_of(i * 256, 256), 256), j * 256:(j + 1) * 256]
            at[j * 256:(j + 1) * 256, pl.ds(pl.multiple_of(i * 256, 256), 256)] = lax.dot_general(
                eye, tile, (((1,), (1,)), ((), ())), preferred_element_type=F32).astype(BF16)
        return carry

    lax.fori_loop(0, 8, flip, 0)

    for dz in (2, 1, 3):
        tz = (me_z + dz) % 4
        w_copy(dz, tz).wait()
        d_copy(tz, core).start()
    for dz in (2, 1, 3):
        tz = (me_z + dz) % 4
        d_copy(tz, core).wait_send()
        d_copy(tz, 1 - core).wait_recv()
    for l in range(layers):
        parts = [wall[q, 0, l].astype(F32) for q in range(4)]
        full = jnp.concatenate([jnp.concatenate(parts, axis=1), jnp.zeros((80, 768), F32)], axis=0)
        wt[l] = jnp.transpose(full).astype(BF16)
        ut[l] = jnp.concatenate([wall[q, 1, l].astype(F32) for q in range(4)], axis=1).astype(BF16)

    @pl.when(jnp.logical_not(inside))
    def _():
        b_copy(0).wait()
        b_copy(1).wait()

    def spot(b):
        tx = (me_x + (7 - b) // 4) % 2
        te = 2 * ((me_e // 2 + (7 - b) // 2) % 2) + (core + 7 - b) % 2
        return tx, te

    def pick(i):
        tx, te = spot(i // 2)
        tl = (low + i + 1) % 2
        return tx, te, tl, te * 4 + tx * 2 + tl

    def c_copy(a, tx, te, tl, slot):
        t = te * 4 + tx * 2 + tl
        return send(hw.at[a, :, pl.ds(pl.multiple_of(t * 128, 128), 128)], recv_c.at[slot, a],
                    sem_cs.at[a, t], sem_cr.at[a, slot], ids(tx, te, 2 * grp + tl))

    def f_copy(a, tx, te, tl, slot):
        t = te * 4 + tx * 2 + tl
        return send(send_f.at[a, t], recv_f.at[a, slot], sem_fs.at[a, t], sem_fr.at[a, slot], ids(tx, te, 2 * grp + tl))

    def o_copy(te, tz, slot):
        t = te * 4 + tz
        return send(out_s.at[t], out_r.at[:, pl.ds(pl.multiple_of(slot * 128, 128), 128)],
                    sem_os.at[t], sem_or.at[slot], ids(grp, te, tz))

    def others(fn):
        def body(i, carry):
            tx, te, tl, t = pick(i)

            @pl.when(t != me)
            def _():
                fn(tx, te, tl, t)
            return carry
        lax.fori_loop(0, 16, body, 0)

    def forecast(cyc, a):
        @pl.when(cyc == 0)
        def _():
            for q in range(4):
                @pl.when(jnp.logical_not(jnp.logical_and(inside, me_z == q)))
                def _():
                    i_arrive(a, q).wait_recv()
            for q in range(4):
                hw[a, q * 12:(q + 1) * 12, :] = r0[a, q]
            hb[0] = hw[a].astype(BF16)

        @pl.when(cyc > 0)
        def _():
            def drain(tx, te, tl, t):
                c_copy(a, tx, te, tl, t).wait_send()
                f_copy(a, tx, te, tl, t).wait()
            others(drain)

            def load(j, carry):
                sl = pl.ds(pl.multiple_of(j * 128, 128), 128)
                block = recv_f[a, j]
                hw[a, :, sl] = block
                hb[0, :, sl] = block.astype(BF16)
                return carry
            lax.fori_loop(0, 16, load, 0)

        pad = jnp.zeros((80, 256), BF16)

        def layer(l, carry):
            now = l % 2
            spots = [spot(b) for b in range(8)]
            slices = [pl.ds(pl.multiple_of((2 * te + tx) * 256, 256), 256) for tx, te in spots]

            def mixed(b):
                res = jnp.dot(hb[now], at[:, slices[b]], preferred_element_type=F32)
                return jnp.concatenate([res.astype(BF16), pad], axis=0)

            def sends(bs):
                @pl.when(l == layers - 1)
                def _():
                    for b in bs:
                        tx, te = spots[b]
                        for tl in range(2):
                            t = te * 4 + tx * 2 + tl

                            @pl.when(t != me)
                            def _():
                                c_copy(a, tx, te, tl, me).start()

                            @pl.when(t == me)
                            def _():
                                recv_c[me, a] = hw[a, :, pl.ds(pl.multiple_of(me * 128, 128), 128)]

            mix = mixed(0)
            for b in range(8):
                following = mixed(b + 1) if b < 7 else None
                parts = []
                for n in range(6):
                    hid = jnp.dot(wt[l, n * 128:(n + 1) * 128, :], mix, preferred_element_type=F32)
                    parts.append(gelu(hid).astype(BF16))
                upd = jnp.dot(ut[l], jnp.concatenate(parts, axis=0), preferred_element_type=F32)
                new = hw[a, :, slices[b]] + upd
                hw[a, :, slices[b]] = new
                hb[1 - now, :, slices[b]] = new.astype(BF16)
                mix = following
                if b == 3:
                    sends(range(4))
            sends(range(4, 8))
            return carry
        lax.fori_loop(0, layers, layer, 0)

    def mat(p_ref, rows):
        out = []
        for i in range(n_obs):
            acc = None
            for k in range(n_obs):
                term = p_ref[i, k:k + 1, :] * rows[k]
                acc = term if acc is None else acc + term
            out.append(acc)
        return out

    def vec(p_ref, x):
        acc = None
        for k in range(n_obs):
            term = x[k:k + 1, :] * p_ref[k]
            acc = term if acc is None else acc + term
        return acc

    sub = lax.broadcasted_iota(jnp.int32, (n_obs, 128), 0)
    units = [jnp.where(sub == i, 1.0, 0.0).astype(F32) for i in range(n_obs)]
    c0 = (members - 1) / rho_ref[0]

    def analyse(cyc):
        for a in range(2):
            others(lambda tx, te, tl, t: c_copy(a, tx, te, tl, t).wait_recv())

        def add(j, acc):
            return acc + (recv_c[j, 0] + recv_c[j, 1])
        mean = lax.fori_loop(0, 16, add, jnp.zeros((48, 128), F32)) * (1.0 / members)
        m_s[...] = mean

        def centre(j, carry):
            for a in range(2):
                recv_c[j, a] = recv_c[j, a] - mean
            return carry
        lax.fori_loop(0, 16, centre, 0)

        root = jnp.sqrt(r_ref[...])
        for p in range(n_obs):
            ip = idx_ref[p]
            v_s[:, :, p:p + 1, :] = recv_c[:, :, pl.ds(ip, 1), :] * root[p:p + 1, :]

        for base_p in range(0, n_obs, 6):
            def outer(j, accs):
                accs = list(accs)
                for a in range(2):
                    x = recv_c[j, a]
                    for p in range(6):
                        accs[p] = accs[p] + v_s[j, a, base_p + p:base_p + p + 1, :] * x
                return tuple(accs)
            sums = lax.fori_loop(0, 16, outer, tuple(jnp.zeros((48, 128), F32) for _ in range(6)))
            for p in range(6):
                f_s[base_p + p] = sums[p]

        gain = []
        for q in range(n_obs):
            iq = idx_ref[q]
            c_m[:, q:q + 1, :] = f_s[:, pl.ds(iq, 1), :] * root[q:q + 1, :]
            gain.append(root[q:q + 1, :] * (y_ref[cyc, q:q + 1, :] - m_s[pl.ds(iq, 1), :]))
        gain = jnp.concatenate(gain, axis=0)

        trace = None
        for p in range(n_obs):
            term = c_m[p, p:p + 1, :]
            trace = term if trace is None else trace + term
        trace = trace + members * c0
        inv = 1.0 / trace
        for p in range(n_obs):
            dn_m[p] = units[p] * inv
            dz_m[p] = jnp.zeros((n_obs, 128), F32)

        def step(i, carry):
            n, z = carry
            t = 1.5 - 0.5 * n
            c_rows = [c_m[k] for k in range(n_obs)]
            nc = mat(dn_m, c_rows)
            for p in range(n_obs):
                t_m[p] = t * units[p] - 0.5 * nc[p]
            tz = mat(t_m, [dz_m[k] for k in range(n_obs)])
            tt = mat(t_m, [t_m[k] for k in range(n_obs)])
            for p in range(n_obs):
                dz_m[p] = tz[p] - (0.5 * z) * dn_m[p]
                q_m[p] = tt[p] - (0.5 * n) * (t_m[p] + t * units[p])
            dn = mat(dn_m, [q_m[k] for k in range(n_obs)])
            for p in range(n_obs):
                dn_m[p] = dn[p]
            return n * t * t, t * z
        n, z = lax.fori_loop(0, NS_STEPS, step, (c0 * inv, jnp.ones((1, 128), F32)))

        rs = 1.0 / jnp.sqrt(trace)
        scale = float((members - 1) ** 0.5) * rs
        alpha = scale * z

        def apply_z(x):
            return z * x + vec(dz_m, vec(c_m, x))
        h = apply_z(apply_z(gain)) * inv

        base = m_s[...]
        for p in range(n_obs):
            base = base + h[p:p + 1, :] * f_s[p]
        m_s[...] = base
        for q in range(n_obs):
            acc = None
            for p in range(n_obs):
                term = (scale * dz_m[q, p:p + 1, :]) * f_s[p]
                acc = term if acc is None else acc + term
            ft_s[q] = acc

        def updated(t, a):
            acc = m_s[...] + alpha * recv_c[t, a]
            for q in range(n_obs):
                acc = acc + v_s[t, a, q:q + 1, :] * ft_s[q]
            return acc

        @pl.when(cyc < cycles - 1)
        def _():
            for a in range(2):
                def back(i, carry):
                    tx, te, tl, t = pick(i)
                    new = updated(t, a)

                    @pl.when(t != me)
                    def _():
                        send_f[a, t] = new
                        f_copy(a, tx, te, tl, me).start()

                    @pl.when(t == me)
                    def _():
                        recv_f[a, me] = new
                    return carry
                lax.fori_loop(0, 16, back, 0)

        @pl.when(cyc == cycles - 1)
        def _():
            def final(i, carry):
                te = (me_e + i) % 4
                for k in range(8):
                    new = updated(te * 4 + k // 2, k % 2)
                    for q in range(4):
                        out_s[te * 4 + q, pl.ds(k, 12, stride=8), :] = new[q * 12:(q + 1) * 12, :]
                for dz in (2, 1, 3, 0):
                    tz = (me_z + dz) % 4
                    own = jnp.logical_and(inside, jnp.logical_and(te == me_e, tz == me_z))

                    @pl.when(jnp.logical_not(own))
                    def _():
                        o_copy(te, tz, me).start()

                    @pl.when(own)
                    def _():
                        out_r[:, pl.ds(pl.multiple_of(me * 128, 128), 128)] = out_s[te * 4 + tz]
                return carry
            lax.fori_loop(0, 4, final, 0)

    def cycle(cyc, carry):
        def one(a, inner):
            forecast(cyc, a)
            return inner
        lax.fori_loop(0, 2, one, 0)
        analyse(cyc)
        return carry
    lax.fori_loop(0, cycles, cycle, 0)

    for a in range(2):
        others(lambda tx, te, tl, t: c_copy(a, tx, te, tl, t).wait_send())
        end_init(a)

    def finish(i, carry):
        own = jnp.logical_and(inside, i == me)

        @pl.when(jnp.logical_not(own))
        def _():
            o_copy(i // 4, i % 4, i).wait_recv()

        @pl.when(jnp.logical_not(jnp.logical_and(inside, i == me_e * 4 + me_z)))
        def _():
            o_copy(i // 4, i % 4, i).wait_send()
        return carry
    lax.fori_loop(0, 16, finish, 0)
    out_ref[...] = out_r[...]


def solution(mesh):
    def local_step(ens_local, mix_op, w_in, w_out, obs_val, obs_prec, obs_idx, inflation):
        cycles, layers = obs_val.shape[0], w_in.shape[0]
        n_obs = obs_idx.shape[0]
        x0 = jnp.transpose(ens_local, (2, 0, 1)).reshape(96, 2048)
        u_t = jnp.transpose(w_out, (0, 2, 1))
        yobs = jnp.transpose(obs_val, (0, 2, 1))
        rinv = jnp.transpose(obs_prec)
        vmem = pl.BlockSpec(memory_space=pltpu.VMEM)
        smem = pl.BlockSpec(memory_space=pltpu.SMEM)
        dma = pltpu.SemaphoreType.DMA
        out = pl.pallas_call(
            functools.partial(kernel, (cycles, layers, n_obs)),
            out_shape=jax.ShapeDtypeStruct((96, 2048), F32),
            in_specs=[smem, smem, vmem, pl.BlockSpec(memory_space=pl.ANY), vmem, vmem, vmem, vmem],
            out_specs=vmem,
            scratch_shapes=[
                pltpu.VMEM((2048, 2048), BF16),
                pltpu.VMEM((2048, 2048), BF16),
                pltpu.VMEM((4, 2, layers, 48, 192), BF16),
                pltpu.VMEM((layers, 768, 128), BF16),
                pltpu.VMEM((layers, 48, 768), BF16),
                pltpu.VMEM((2, 4, 12, 2048), F32),
                pltpu.VMEM((2, 4, 12, 2048), F32),
                pltpu.VMEM((2, 2, 12, 2048), F32),
                pltpu.VMEM((cycles, n_obs, 128), F32),
                pltpu.VMEM((n_obs, 128), F32),
                pltpu.VMEM((2, 48, 2048), F32),
                pltpu.VMEM((2, 48, 2048), BF16),
                pltpu.VMEM((16, 2, 48, 128), F32),
                pltpu.VMEM((2, 16, 48, 128), F32),
                pltpu.VMEM((2, 16, 48, 128), F32),
                pltpu.VMEM((16, 96, 128), F32),
                pltpu.VMEM((96, 2048), F32),
                pltpu.VMEM((16, 2, n_obs, 128), F32),
                pltpu.VMEM((n_obs, 48, 128), F32),
                pltpu.VMEM((n_obs, 48, 128), F32),
                pltpu.VMEM((48, 128), F32),
                pltpu.VMEM((n_obs, n_obs, 128), F32),
                pltpu.VMEM((n_obs, n_obs, 128), F32),
                pltpu.VMEM((n_obs, n_obs, 128), F32),
                pltpu.VMEM((n_obs, n_obs, 128), F32),
                pltpu.VMEM((n_obs, n_obs, 128), F32),
                dma(()),
                dma((4,)), dma((4,)), dma((4,)), dma((4,)), dma((2,)), dma((2,)),
                dma((2, 4)), dma((2, 4)), dma((2, 2)), dma((2, 2)),
                dma((2, 16)), dma((2, 16)),
                dma((2, 16)), dma((2, 16)),
                dma((16,)), dma((16,)),
            ],
            compiler_params=pltpu.CompilerParams(
                collective_id=0, has_side_effects=True, vmem_limit_bytes=60 * 1024 * 1024),
        )(obs_idx, inflation, x0, mix_op, w_in, u_t, yobs, rinv)
        return jnp.transpose(out.reshape(12, 8, 2048), (1, 2, 0))

    member_spec = P(("case", "ens"), None, "model")
    col_axes = ("case", "ens", "model")
    in_specs = (member_spec, P(None, None), P(None, None, "model"), P(None, "model", None), P(None, col_axes, None), P(col_axes, None), P(None), P(None))
    return jax.shard_map(local_step, mesh=mesh, in_specs=in_specs, out_specs=member_spec, check_vma=False)
```

time: 235 us -> 195 us (0.83)
  Pallas kernels: 228 us -> 191 us
    pallas_call x1, Pallas kernels: 228 us -> 191 us  [local_step(): pl.pallas_call(functools.partial(kernel, (cycles, layers, n_obs)), out_sh...]
where the time goes in v2:
time: 195 us; the launch traced here: 194 us
  Pallas kernels  191 us (98%)
  local copies, waits for them, and re-layouts  2.06 us (1%)
    pallas_call x1, Pallas kernels, local_step(): pl.pallas_call(functools.partial(kernel, (cycles, layers, n_obs)), out_sh...  191 us

profile of v2, /device:TPU:2, one launch (start us, length us, event | category | flops | bytes accessed | tf_op | source)
XLA Modules:
  0.0 194.1 jit_solution(5025232963219926092)
XLA Ops:
  0.7 191.4 %shard_map.82 = f32[96,2048]{1,0:T(8,128)} custom-call(s32[12]{0:T(128)} %idx_ref.1, f32[1]{0:T(128)S(6)} %copy.10.rho_ref, f32[96,2048]{1,0:T(8,128)} %bitcast.10, bf16[2048,2048]{1,0:T(8,128)(2,1)} %a_hbm.1, bf16[3,48,192]{2,1,0:T(8,128)(2,1)} %w_ref.1, bf16[3,48,192]{2,1,0:T(8,128)(2,1)} %bitcast.11, f32[3,12,128]{2,1,0:T(8,128)} %bitcast.12, ...), custom_call_target="tpu_custom_call" | custom-call | tf_op jit(solution)/shard_map/pallas_call | solution.py:476
  192.0 2.1 %copy.11 = f32[8,2048,12]{1,0,2:T(8,128)} copy(f32[8,2048,12]{1,0,2:T(8,128)} %bitcast.9) | data formatting | bytes 1572864

commit v3 on v2

--- a/solution.py
+++ b/solution.py
@@ -22,9 +22,9 @@
 
 
 def kernel(dims, idx_ref, rho_ref, x0_ref, a_hbm, w_ref, u_ref, y_in, r_in, out_ref,
-           a_v, at, wall, wt, ut, s0, r0, relay, y_ref, r_ref, hw, hb, recv_c, recv_f, send_f, out_s, out_r,
+           a_v, at, wall, wt, ut, s0, r0, relay, y_ref, r_ref, hw, hb, mt, recv_c, recv_f, send_f, out_s, out_r,
            v_s, f_s, ft_s, m_s, c_m, dn_m, dz_m, t_m, q_m,
-           sem_a, sem_ws, sem_wr, sem_ds, sem_dr, sem_bs, sem_br, sem_is, sem_ir, sem_rs, sem_rr,
+           sem_a, sem_zs, sem_wr, sem_hs, sem_vs, sem_ds, sem_dr, sem_bs, sem_br, sem_is, sem_ir, sem_rs, sem_rr,
            sem_cs, sem_cr, sem_fs, sem_fr, sem_os, sem_or):
     cycles, layers, n_obs = dims
     me_x = lax.axis_index("case")
@@ -80,12 +80,73 @@
         dev = ids(me_z // 2, me_e, 2 * me_x + low)
         return send(y_in, y_ref, sem_bs.at[0], sem_br.at[0], dev) if n == 0 else send(r_in, r_ref, sem_bs.at[1], sem_br.at[1], dev)
 
-    def w_copy(dz, slot):
+    def home(l):
+        return me_x == l % 2, me_e // 2 == (l // 2) % 2
+
+    def z_copy(l, dz, slot):
         tz = (me_z + dz) % 4
-        return send(wall.at[me_z, core], wall.at[slot, core], sem_ws.at[tz], sem_wr.at[slot], ids(me_x, me_e, tz))
+        return send(wall.at[me_z, core, l], wall.at[slot, core, l], sem_zs.at[l, tz], sem_wr.at[l, slot], ids(me_x, me_e, tz))
+
+    def h_copy(l, q):
+        return send(wall.at[q, core, l], wall.at[q, core, l], sem_hs.at[l, q], sem_wr.at[l, q], ids(far, me_e, me_z))
+
+    def v_copy(l, q):
+        return send(wall.at[q, core, l], wall.at[q, core, l], sem_vs.at[l, q], sem_wr.at[l, q], ids(me_x, (me_e + 2) % 4, me_z))
 
     def d_copy(q, c):
         return send(wall.at[q, c], wall.at[q, c], sem_ds.at[q], sem_dr.at[q], ids(me_x, mate, me_z))
+
+    shifts = (2, 1, 3)
+
+    def w_stage(stage):
+        for l in range(layers):
+            on_x, on_y = home(l)
+            away = jnp.logical_not(on_x)
+            off = jnp.logical_not(on_y)
+            first = jnp.logical_and(on_x, on_y)
+            second = jnp.logical_and(away, on_y)
+            if stage == 0:
+                @pl.when(first)
+                def _():
+                    for dz in shifts:
+                        z_copy(l, dz, me_z).start()
+            if stage == 1:
+                @pl.when(first)
+                def _():
+                    for dz in shifts:
+                        q = (me_z + dz) % 4
+                        z_copy(l, dz, q).wait()
+                        h_copy(l, q).start()
+                        v_copy(l, q).start()
+            if stage == 2:
+                @pl.when(second)
+                def _():
+                    for dz in shifts:
+                        q = (me_z + dz) % 4
+                        h_copy(l, q).wait_recv()
+                        v_copy(l, q).start()
+            if stage == 3:
+                @pl.when(off)
+                def _():
+                    for dz in shifts:
+                        v_copy(l, (me_z + dz) % 4).wait_recv()
+
+                @pl.when(first)
+                def _():
+                    for dz in shifts:
+                        h_copy(l, (me_z + dz) % 4).wait_send()
+
+                @pl.when(on_y)
+                def _():
+                    for dz in shifts:
+                        v_copy(l, (me_z + dz) % 4).wait_send()
+        if stage == 3:
+            for dz in shifts:
+                d_copy((me_z + dz) % 4, core).start()
+            for dz in shifts:
+                q = (me_z + dz) % 4
+                d_copy(q, core).wait_send()
+                d_copy(q, 1 - core).wait_recv()
 
     def start_init(a):
         @pl.when(inside)
@@ -126,11 +187,8 @@
                 x_copy(a, k).wait_send()
                 i_copy(a, 2 * me_x + k).wait_send()
 
+    w_stage(0)
     start_init(0)
-    for dz in (2, 1, 3):
-        w_copy(dz, me_z).start()
-    start_relay(0)
-    start_init(1)
 
     @pl.when(inside)
     def _():
@@ -141,7 +199,7 @@
     def _():
         b_copy(0).start()
         b_copy(1).start()
-    start_relay(1)
+    mt[48:128, :] = jnp.zeros((80, 2048), BF16)
 
     copy_a.wait()
     row = lax.broadcasted_iota(jnp.int32, (256, 256), 0)
@@ -155,16 +213,14 @@
                 eye, tile, (((1,), (1,)), ((), ())), preferred_element_type=F32).astype(BF16)
         return carry
 
+    w_stage(1)
+    start_relay(0)
+    w_stage(2)
+    start_init(1)
     lax.fori_loop(0, 8, flip, 0)
-
-    for dz in (2, 1, 3):
-        tz = (me_z + dz) % 4
-        w_copy(dz, tz).wait()
-        d_copy(tz, core).start()
-    for dz in (2, 1, 3):
-        tz = (me_z + dz) % 4
-        d_copy(tz, core).wait_send()
-        d_copy(tz, 1 - core).wait_recv()
+    w_stage(3)
+    start_relay(1)
+
     for l in range(layers):
         parts = [wall[q, 0, l].astype(F32) for q in range(4)]
         full = jnp.concatenate([jnp.concatenate(parts, axis=1), jnp.zeros((80, 768), F32)], axis=0)
@@ -219,7 +275,7 @@
                     i_arrive(a, q).wait_recv()
             for q in range(4):
                 hw[a, q * 12:(q + 1) * 12, :] = r0[a, q]
-            hb[0] = hw[a].astype(BF16)
+            hb[...] = hw[a].astype(BF16)
 
         @pl.when(cyc > 0)
         def _():
@@ -232,54 +288,47 @@
                 sl = pl.ds(pl.multiple_of(j * 128, 128), 128)
                 block = recv_f[a, j]
                 hw[a, :, sl] = block
-                hb[0, :, sl] = block.astype(BF16)
+                hb[:, sl] = block.astype(BF16)
                 return carry
             lax.fori_loop(0, 16, load, 0)
 
-        pad = jnp.zeros((80, 256), BF16)
+        def mix_all():
+            for n in range(2):
+                sl = slice(n * 1024, (n + 1) * 1024)
+                mt[0:48, sl] = jnp.dot(hb[...], at[:, sl], preferred_element_type=F32).astype(BF16)
+
+        def tile(l, sl):
+            mix = mt[:, sl]
+            parts = []
+            for n in range(6):
+                hid = jnp.dot(wt[l, n * 128:(n + 1) * 128, :], mix, preferred_element_type=F32)
+                parts.append(gelu(hid).astype(BF16))
+            upd = jnp.dot(ut[l], jnp.concatenate(parts, axis=0), preferred_element_type=F32)
+            new = hw[a, :, sl] + upd
+            hw[a, :, sl] = new
+            return new
 
         def layer(l, carry):
-            now = l % 2
-            spots = [spot(b) for b in range(8)]
-            slices = [pl.ds(pl.multiple_of((2 * te + tx) * 256, 256), 256) for tx, te in spots]
-
-            def mixed(b):
-                res = jnp.dot(hb[now], at[:, slices[b]], preferred_element_type=F32)
-                return jnp.concatenate([res.astype(BF16), pad], axis=0)
-
-            def sends(bs):
-                @pl.when(l == layers - 1)
-                def _():
-                    for b in bs:
-                        tx, te = spots[b]
-                        for tl in range(2):
-                            t = te * 4 + tx * 2 + tl
-
-                            @pl.when(t != me)
-                            def _():
-                                c_copy(a, tx, te, tl, me).start()
-
-                            @pl.when(t == me)
-                            def _():
-                                recv_c[me, a] = hw[a, :, pl.ds(pl.multiple_of(me * 128, 128), 128)]
-
-            mix = mixed(0)
+            mix_all()
             for b in range(8):
-                following = mixed(b + 1) if b < 7 else None
-                parts = []
-                for n in range(6):
-                    hid = jnp.dot(wt[l, n * 128:(n + 1) * 128, :], mix, preferred_element_type=F32)
-                    parts.append(gelu(hid).astype(BF16))
-                upd = jnp.dot(ut[l], jnp.concatenate(parts, axis=0), preferred_element_type=F32)
-                new = hw[a, :, slices[b]] + upd
-                hw[a, :, slices[b]] = new
-                hb[1 - now, :, slices[b]] = new.astype(BF16)
-                mix = following
-                if b == 3:
-                    sends(range(4))
-            sends(range(4, 8))
+                sl = slice(b * 256, (b + 1) * 256)
+                hb[:, sl] = tile(l, sl).astype(BF16)
             return carry
-        lax.fori_loop(0, layers, layer, 0)
+        lax.fori_loop(0, layers - 1, layer, 0)
+
+        def sends(b):
+            tx, te = spot(b)
+            for tl in ((1 - low, low) if b < 7 else (1 - low,)):
+                c_copy(a, tx, te, tl, me).start()
+
+        mix_all()
+        for b in range(8):
+            tx, te = spot(b)
+            tile(layers - 1, pl.ds(pl.multiple_of((2 * te + tx) * 256, 256), 256))
+            if b % 4 == 3:
+                for n in range(b - 3, b + 1):
+                    sends(n)
+        recv_c[me, a] = hw[a, :, pl.ds(pl.multiple_of(me * 128, 128), 128)]
 
     def mat(p_ref, rows):
         out = []
@@ -347,27 +396,37 @@
             trace = term if trace is None else trace + term
         trace = trace + members * c0
         inv = 1.0 / trace
+        n0 = c0 * inv
+        t0 = 1.5 - 0.5 * n0
         for p in range(n_obs):
-            dn_m[p] = units[p] * inv
-            dz_m[p] = jnp.zeros((n_obs, 128), F32)
-
-        def step(i, carry):
-            n, z = carry
+            dz_m[p] = units[p] * (-0.5 * inv)
+            t_m[p] = t0 * units[p] - (0.5 * inv) * c_m[p]
+        tt = mat(t_m, [t_m[k] for k in range(n_obs)])
+        for p in range(n_obs):
+            dn_m[p] = inv * (tt[p] - (0.5 * n0) * (t_m[p] + t0 * units[p]))
+
+        def half_step(n, z):
             t = 1.5 - 0.5 * n
-            c_rows = [c_m[k] for k in range(n_obs)]
-            nc = mat(dn_m, c_rows)
+            nc = mat(dn_m, [c_m[k] for k in range(n_obs)])
             for p in range(n_obs):
                 t_m[p] = t * units[p] - 0.5 * nc[p]
             tz = mat(t_m, [dz_m[k] for k in range(n_obs)])
+            for p in range(n_obs):
+                dz_m[p] = tz[p] - (0.5 * z) * dn_m[p]
+            return t
+
+        def step(i, carry):
+            n, z = carry
+            t = half_step(n, z)
             tt = mat(t_m, [t_m[k] for k in range(n_obs)])
             for p in range(n_obs):
-                dz_m[p] = tz[p] - (0.5 * z) * dn_m[p]
                 q_m[p] = tt[p] - (0.5 * n) * (t_m[p] + t * units[p])
             dn = mat(dn_m, [q_m[k] for k in range(n_obs)])
             for p in range(n_obs):
                 dn_m[p] = dn[p]
             return n * t * t, t * z
-        n, z = lax.fori_loop(0, NS_STEPS, step, (c0 * inv, jnp.ones((1, 128), F32)))
+        n, z = lax.fori_loop(1, NS_STEPS - 1, step, (n0 * t0 * t0, t0))
+        z = half_step(n, z) * z
 
         rs = 1.0 / jnp.sqrt(trace)
         scale = float((members - 1) ** 0.5) * rs
@@ -490,7 +549,8 @@
                 pltpu.VMEM((cycles, n_obs, 128), F32),
                 pltpu.VMEM((n_obs, 128), F32),
                 pltpu.VMEM((2, 48, 2048), F32),
-                pltpu.VMEM((2, 48, 2048), BF16),
+                pltpu.VMEM((48, 2048), BF16),
+                pltpu.VMEM((128, 2048), BF16),
                 pltpu.VMEM((16, 2, 48, 128), F32),
                 pltpu.VMEM((2, 16, 48, 128), F32),
                 pltpu.VMEM((2, 16, 48, 128), F32),
@@ -506,7 +566,8 @@
                 pltpu.VMEM((n_obs, n_obs, 128), F32),
                 pltpu.VMEM((n_obs, n_obs, 128), F32),
                 dma(()),
-                dma((4,)), dma((4,)), dma((4,)), dma((4,)), dma((2,)), dma((2,)),
+                dma((layers, 4)), dma((layers, 4)), dma((layers, 4)), dma((layers, 4)),
+                dma((4,)), dma((4,)), dma((2,)), dma((2,)),
                 dma((2, 4)), dma((2, 4)), dma((2, 2)), dma((2, 2)),
                 dma((2, 16)), dma((2, 16)),
                 dma((2, 16)), dma((2, 16)),

time: 195 us -> 179 us (0.918)
  Pallas kernels: 191 us -> 176 us
    pallas_call x1, Pallas kernels: 191 us -> 176 us  [local_step(): pl.pallas_call(functools.partial(kernel, (cycles, layers, n_obs)), out_sh...]
where the time goes in v3:
time: 179 us
  Pallas kernels  176 us (98%)
  local copies, waits for them, and re-layouts  2.06 us (1%)
    pallas_call x1, Pallas kernels, local_step(): pl.pallas_call(functools.partial(kernel, (cycles, layers, n_obs)), out_sh...  176 us

profile of v3, /device:TPU:2, one launch (start us, length us, event | category | flops | bytes accessed | tf_op | source)
XLA Modules:
  0.0 178.9 jit_solution(6787581324426373857)
XLA Ops:
  0.7 176.1 %shard_map.82 = f32[96,2048]{1,0:T(8,128)} custom-call(s32[12]{0:T(128)} %idx_ref.1, f32[1]{0:T(128)S(6)} %copy.10.rho_ref, f32[96,2048]{1,0:T(8,128)} %bitcast.10, bf16[2048,2048]{1,0:T(8,128)(2,1)} %a_hbm.1, bf16[3,48,192]{2,1,0:T(8,128)(2,1)} %w_ref.1, bf16[3,48,192]{2,1,0:T(8,128)(2,1)} %bitcast.11, f32[3,12,128]{2,1,0:T(8,128)} %bitcast.12, ...), custom_call_target="tpu_custom_call" | custom-call | tf_op jit(solution)/shard_map/pallas_call | solution.py:535
  176.8 2.1 %copy.11 = f32[8,2048,12]{1,0,2:T(8,128)} copy(f32[8,2048,12]{1,0,2:T(8,128)} %bitcast.9) | data formatting | bytes 1572864

commit v4 on v3

--- a/solution.py
+++ b/solution.py
@@ -23,7 +23,7 @@
 
 def kernel(dims, idx_ref, rho_ref, x0_ref, a_hbm, w_ref, u_ref, y_in, r_in, out_ref,
            a_v, at, wall, wt, ut, s0, r0, relay, y_ref, r_ref, hw, hb, mt, recv_c, recv_f, send_f, out_s, out_r,
-           v_s, f_s, ft_s, m_s, c_m, dn_m, dz_m, t_m, q_m,
+           x_s, v_s, f_s, ft_s, m_s, d_s, b_s, c_m, dn_m, dz_m, t_m, q_m,
            sem_a, sem_zs, sem_wr, sem_hs, sem_vs, sem_ds, sem_dr, sem_bs, sem_br, sem_is, sem_ir, sem_rs, sem_rr,
            sem_cs, sem_cr, sem_fs, sem_fr, sem_os, sem_or):
     cycles, layers, n_obs = dims
@@ -245,26 +245,25 @@
     def c_copy(a, tx, te, tl, slot):
         t = te * 4 + tx * 2 + tl
         return send(hw.at[a, :, pl.ds(pl.multiple_of(t * 128, 128), 128)], recv_c.at[slot, a],
-                    sem_cs.at[a, t], sem_cr.at[a, slot], ids(tx, te, 2 * grp + tl))
+                    sem_cs.at[a], sem_cr.at[a], ids(tx, te, 2 * grp + tl))
 
     def f_copy(a, tx, te, tl, slot):
         t = te * 4 + tx * 2 + tl
-        return send(send_f.at[a, t], recv_f.at[a, slot], sem_fs.at[a, t], sem_fr.at[a, slot], ids(tx, te, 2 * grp + tl))
+        return send(send_f.at[a, t], recv_f.at[a, slot], sem_fs.at[a], sem_fr.at[a], ids(tx, te, 2 * grp + tl))
 
     def o_copy(te, tz, slot):
         t = te * 4 + tz
         return send(out_s.at[t], out_r.at[:, pl.ds(pl.multiple_of(slot * 128, 128), 128)],
-                    sem_os.at[t], sem_or.at[slot], ids(grp, te, tz))
-
-    def others(fn):
-        def body(i, carry):
-            tx, te, tl, t = pick(i)
-
-            @pl.when(t != me)
-            def _():
-                fn(tx, te, tl, t)
-            return carry
-        lax.fori_loop(0, 16, body, 0)
+                    sem_os, sem_or, ids(grp, te, tz))
+
+    def c_all(a):
+        return send(recv_c.at[0:15, a], recv_c.at[0:15, a], sem_cs.at[a], sem_cr.at[a], ids(far, me_e, me_z))
+
+    def f_all(a):
+        return send(send_f.at[a, 0:15], recv_f.at[a, 0:15], sem_fs.at[a], sem_fr.at[a], ids(far, me_e, me_z))
+
+    def o_all(n):
+        return send(out_s.at[0:n], out_s.at[0:n], sem_os, sem_or, ids(far, me_e, me_z))
 
     def forecast(cyc, a):
         @pl.when(cyc == 0)
@@ -279,18 +278,13 @@
 
         @pl.when(cyc > 0)
         def _():
-            def drain(tx, te, tl, t):
-                c_copy(a, tx, te, tl, t).wait_send()
-                f_copy(a, tx, te, tl, t).wait()
-            others(drain)
-
-            def load(j, carry):
-                sl = pl.ds(pl.multiple_of(j * 128, 128), 128)
+            c_all(a).wait_send()
+            f_all(a).wait()
+            for j in range(16):
+                sl = slice(j * 128, (j + 1) * 128)
                 block = recv_f[a, j]
                 hw[a, :, sl] = block
                 hb[:, sl] = block.astype(BF16)
-                return carry
-            lax.fori_loop(0, 16, load, 0)
 
         def mix_all():
             for n in range(2):
@@ -352,36 +346,48 @@
     c0 = (members - 1) / rho_ref[0]
 
     def analyse(cyc):
+        root = jnp.sqrt(r_ref[...])
+        means = []
         for a in range(2):
-            others(lambda tx, te, tl, t: c_copy(a, tx, te, tl, t).wait_recv())
-
-        def add(j, acc):
-            return acc + (recv_c[j, 0] + recv_c[j, 1])
-        mean = lax.fori_loop(0, 16, add, jnp.zeros((48, 128), F32)) * (1.0 / members)
+            c_all(a).wait_recv()
+
+            def add(j, acc):
+                return acc + ((recv_c[4 * j, a] + recv_c[4 * j + 1, a]) + (recv_c[4 * j + 2, a] + recv_c[4 * j + 3, a]))
+            part = lax.fori_loop(0, 4, add, jnp.zeros((48, 128), F32)) * (2.0 / members)
+            means.append(part)
+
+            def centre(j, carry):
+                for n in range(4):
+                    block = recv_c[4 * j + n, a] - part
+                    recv_c[4 * j + n, a] = block
+                    x_s[4 * j + n] = block
+                return carry
+            lax.fori_loop(0, 4, centre, 0)
+
+            for p in range(n_obs):
+                ip = idx_ref[p]
+                v_s[:, a, p:p + 1, :] = x_s[:, pl.ds(ip, 1), :] * root[p:p + 1, :]
+
+            for base_p in range(0, n_obs, 6):
+                def outer(j, accs):
+                    accs = list(accs)
+                    for n in range(2):
+                        x = recv_c[2 * j + n, a]
+                        for p in range(6):
+                            accs[p] = accs[p] + v_s[2 * j + n, a, base_p + p:base_p + p + 1, :] * x
+                    return tuple(accs)
+                start = tuple(jnp.zeros((48, 128), F32) if a == 0 else f_s[base_p + p] for p in range(6))
+                sums = lax.fori_loop(0, 8, outer, start)
+                for p in range(6):
+                    f_s[base_p + p] = sums[p]
+
+        mean = 0.5 * (means[0] + means[1])
+        delta = 0.5 * (means[0] - means[1])
         m_s[...] = mean
-
-        def centre(j, carry):
-            for a in range(2):
-                recv_c[j, a] = recv_c[j, a] - mean
-            return carry
-        lax.fori_loop(0, 16, centre, 0)
-
-        root = jnp.sqrt(r_ref[...])
+        d_s[...] = delta
+        shift = [root[p:p + 1, :] * d_s[pl.ds(idx_ref[p], 1), :] for p in range(n_obs)]
         for p in range(n_obs):
-            ip = idx_ref[p]
-            v_s[:, :, p:p + 1, :] = recv_c[:, :, pl.ds(ip, 1), :] * root[p:p + 1, :]
-
-        for base_p in range(0, n_obs, 6):
-            def outer(j, accs):
-                accs = list(accs)
-                for a in range(2):
-                    x = recv_c[j, a]
-                    for p in range(6):
-                        accs[p] = accs[p] + v_s[j, a, base_p + p:base_p + p + 1, :] * x
-                return tuple(accs)
-            sums = lax.fori_loop(0, 16, outer, tuple(jnp.zeros((48, 128), F32) for _ in range(6)))
-            for p in range(6):
-                f_s[base_p + p] = sums[p]
+            f_s[p] = f_s[p] + (float(members) * shift[p]) * delta
 
         gain = []
         for q in range(n_obs):
@@ -439,16 +445,19 @@
         base = m_s[...]
         for p in range(n_obs):
             base = base + h[p:p + 1, :] * f_s[p]
-        m_s[...] = base
+        move = alpha * d_s[...]
         for q in range(n_obs):
             acc = None
             for p in range(n_obs):
                 term = (scale * dz_m[q, p:p + 1, :]) * f_s[p]
                 acc = term if acc is None else acc + term
             ft_s[q] = acc
+            move = move + shift[q] * acc
+        b_s[0] = base + move
+        b_s[1] = base - move
 
         def updated(t, a):
-            acc = m_s[...] + alpha * recv_c[t, a]
+            acc = b_s[a] + alpha * recv_c[t, a]
             for q in range(n_obs):
                 acc = acc + v_s[t, a, q:q + 1, :] * ft_s[q]
             return acc
@@ -456,20 +465,16 @@
         @pl.when(cyc < cycles - 1)
         def _():
             for a in range(2):
-                def back(i, carry):
-                    tx, te, tl, t = pick(i)
-                    new = updated(t, a)
-
-                    @pl.when(t != me)
-                    def _():
-                        send_f[a, t] = new
+                def back(g, carry):
+                    for n in range(3):
+                        tx, te, tl, t = pick(3 * g + n)
+                        send_f[a, t] = updated(t, a)
+                    for n in range(3):
+                        tx, te, tl, t = pick(3 * g + n)
                         f_copy(a, tx, te, tl, me).start()
-
-                    @pl.when(t == me)
-                    def _():
-                        recv_f[a, me] = new
                     return carry
-                lax.fori_loop(0, 16, back, 0)
+                lax.fori_loop(0, 5, back, 0)
+                recv_f[a, me] = updated(me, a)
 
         @pl.when(cyc == cycles - 1)
         def _():
@@ -503,21 +508,16 @@
     lax.fori_loop(0, cycles, cycle, 0)
 
     for a in range(2):
-        others(lambda tx, te, tl, t: c_copy(a, tx, te, tl, t).wait_send())
+        c_all(a).wait_send()
         end_init(a)
 
-    def finish(i, carry):
-        own = jnp.logical_and(inside, i == me)
-
-        @pl.when(jnp.logical_not(own))
-        def _():
-            o_copy(i // 4, i % 4, i).wait_recv()
-
-        @pl.when(jnp.logical_not(jnp.logical_and(inside, i == me_e * 4 + me_z)))
-        def _():
-            o_copy(i // 4, i % 4, i).wait_send()
-        return carry
-    lax.fori_loop(0, 16, finish, 0)
+    @pl.when(inside)
+    def _():
+        o_all(15).wait()
+
+    @pl.when(jnp.logical_not(inside))
+    def _():
+        o_all(16).wait()
     out_ref[...] = out_r[...]
 
 
@@ -556,10 +556,13 @@
                 pltpu.VMEM((2, 16, 48, 128), F32),
                 pltpu.VMEM((16, 96, 128), F32),
                 pltpu.VMEM((96, 2048), F32),
+                pltpu.VMEM((16, 48, 128), F32),
                 pltpu.VMEM((16, 2, n_obs, 128), F32),
                 pltpu.VMEM((n_obs, 48, 128), F32),
                 pltpu.VMEM((n_obs, 48, 128), F32),
                 pltpu.VMEM((48, 128), F32),
+                pltpu.VMEM((48, 128), F32),
+                pltpu.VMEM((2, 48, 128), F32),
                 pltpu.VMEM((n_obs, n_obs, 128), F32),
                 pltpu.VMEM((n_obs, n_obs, 128), F32),
                 pltpu.VMEM((n_obs, n_obs, 128), F32),
@@ -569,9 +572,9 @@
                 dma((layers, 4)), dma((layers, 4)), dma((layers, 4)), dma((layers, 4)),
                 dma((4,)), dma((4,)), dma((2,)), dma((2,)),
                 dma((2, 4)), dma((2, 4)), dma((2, 2)), dma((2, 2)),
-                dma((2, 16)), dma((2, 16)),
-                dma((2, 16)), dma((2, 16)),
-                dma((16,)), dma((16,)),
+                dma((2,)), dma((2,)),
+                dma((2,)), dma((2,)),
+                dma(()), dma(()),
             ],
             compiler_params=pltpu.CompilerParams(
                 collective_id=0, has_side_effects=True, vmem_limit_bytes=60 * 1024 * 1024),

time: 179 us -> 175 us (0.978)
  Pallas kernels: 176 us -> 172 us
    pallas_call x1, Pallas kernels: 176 us -> 172 us  [local_step(): pl.pallas_call(functools.partial(kernel, (cycles, layers, n_obs)), out_sh...]
where the time goes in v4:
time: 175 us
  Pallas kernels  172 us (98%)
  local copies, waits for them, and re-layouts  2.06 us (1%)
    pallas_call x1, Pallas kernels, local_step(): pl.pallas_call(functools.partial(kernel, (cycles, layers, n_obs)), out_sh...  172 us

profile of v4, /device:TPU:2, one launch (start us, length us, event | category | flops | bytes accessed | tf_op | source)
XLA Modules:
  0.0 174.6 jit_solution(6174754401344418633)
XLA Ops:
  0.7 171.8 %shard_map.82 = f32[96,2048]{1,0:T(8,128)} custom-call(s32[12]{0:T(128)} %idx_ref.1, f32[1]{0:T(128)S(6)} %copy.10.rho_ref, f32[96,2048]{1,0:T(8,128)} %bitcast.10, bf16[2048,2048]{1,0:T(8,128)(2,1)} %a_hbm.1, bf16[3,48,192]{2,1,0:T(8,128)(2,1)} %w_ref.1, bf16[3,48,192]{2,1,0:T(8,128)(2,1)} %bitcast.11, f32[3,12,128]{2,1,0:T(8,128)} %bitcast.12, ...), custom_call_target="tpu_custom_call" | custom-call | tf_op jit(solution)/shard_map/pallas_call | solution.py:535
  172.5 2.1 %copy.11 = f32[8,2048,12]{1,0,2:T(8,128)} copy(f32[8,2048,12]{1,0,2:T(8,128)} %bitcast.9) | data formatting | bytes 1572864

commit v5 on v4

--- a/solution.py
+++ b/solution.py
@@ -319,8 +319,8 @@
         for b in range(8):
             tx, te = spot(b)
             tile(layers - 1, pl.ds(pl.multiple_of((2 * te + tx) * 256, 256), 256))
-            if b % 4 == 3:
-                for n in range(b - 3, b + 1):
+            if b in (4, 7):
+                for n in (range(5) if b == 4 else range(5, 8)):
                     sends(n)
         recv_c[me, a] = hw[a, :, pl.ds(pl.multiple_of(me * 128, 128), 128)]
 

time: 175 us -> 174 us (level)
  no operation moved by 1% of the time
where the time goes in v5:
time: 174 us
  Pallas kernels  171 us (98%)
  local copies, waits for them, and re-layouts  2.06 us (1%)
    pallas_call x1, Pallas kernels, local_step(): pl.pallas_call(functools.partial(kernel, (cycles, layers, n_obs)), out_sh...  171 us

profile of v5, /device:TPU:2, one launch (start us, length us, event | category | flops | bytes accessed | tf_op | source)
XLA Modules:
  0.0 173.6 jit_solution(9386747838626101860)
XLA Ops:
  0.7 170.9 %shard_map.82 = f32[96,2048]{1,0:T(8,128)} custom-call(s32[12]{0:T(128)} %idx_ref.1, f32[1]{0:T(128)S(6)} %copy.10.rho_ref, f32[96,2048]{1,0:T(8,128)} %bitcast.10, bf16[2048,2048]{1,0:T(8,128)(2,1)} %a_hbm.1, bf16[3,48,192]{2,1,0:T(8,128)(2,1)} %w_ref.1, bf16[3,48,192]{2,1,0:T(8,128)(2,1)} %bitcast.11, f32[3,12,128]{2,1,0:T(8,128)} %bitcast.12, ...), custom_call_target="tpu_custom_call" | custom-call | tf_op jit(solution)/shard_map/pallas_call | solution.py:535
  171.5 2.1 %copy.11 = f32[8,2048,12]{1,0,2:T(8,128)} copy(f32[8,2048,12]{1,0,2:T(8,128)} %bitcast.9) | data formatting | bytes 1572864
